TPU v7x, 32 devices: a whole 2x2x4 slice. The times are simulated.
32 devices in a mesh: grp: 2 (over x), lon: 4 (over y, core), lat: 4 (over z).
Axes of the slice: x: 2, y: 2, z: 4, core: 2. Of those that a mesh axis runs over, the one named last changes fastest.
Arguments:
- fields: bfloat16 [6, 2, 48, 48, 512], P('grp', None, 'lat', 'lon'), may hold values from -6 to 6
- surface_mask: int32 [2, 48, 48], P(None, 'lat', 'lon'), may hold values 0 or 1
- w_qkv: bfloat16 [512, 1536], replicated, may hold values from -0.25 to 0.25
- w_out: bfloat16 [512, 512], replicated, may hold values from -0.25 to 0.25
- logit_scale: float32 [8], replicated, may hold values from 2 to 12
- mask_bias: float32 [8], replicated, may hold values from -2 to 2
- w_up: bfloat16 [512, 2048], replicated, may hold values from -0.25 to 0.25
- w_down: bfloat16 [2048, 512], replicated, may hold values from -0.125 to 0.125
Outputs:
- joined: bfloat16 [6, 2, 48, 48, 512], P('grp', None, 'lat', 'lon')
All inputs are finite; a program needn't handle non-finite values. No bound on the sum of `surface_mask` on one device may be relied on, other than what follows from the above.
Results may differ from a plain program's by a relative error of at most 0.006.
Values may be sent and summed in bfloat16 or wider, within the bound.
A program may use at most 128 MiB of HBM per device.

v0:
```python
import jax
import jax.numpy as jnp
from jax import lax
from jax.sharding import PartitionSpec as P

WLAT = 6
SH_LAT = 3
SH_LON = 6


def passed_along(array, axis, by):
    count = lax.axis_size(axis)
    return lax.ppermute(array, axis, [(i, (i + by) % count) for i in range(count)])


def layer_norm(values):
    centred = values - jnp.mean(values, -1, keepdims=True)
    return centred * lax.rsqrt(jnp.mean(centred * centred, -1, keepdims=True) + 1e-05)


def unit_heads(mixed_part, head_count):
    shaped = mixed_part.reshape(mixed_part.shape[0], head_count, -1)
    scaled = shaped * lax.rsqrt(jnp.mean(shaped * shaped, -1, keepdims=True) + 1e-06)
    return scaled.reshape(mixed_part.shape).astype(jnp.bfloat16)


def project_heads(tokens_in, w_qkv, head_count):
    model_width = tokens_in.shape[-1]
    normed = layer_norm(tokens_in.astype(jnp.float32)).astype(jnp.bfloat16)
    mixed = jnp.dot(normed.reshape(-1, model_width), w_qkv, preferred_element_type=jnp.float32)
    queries = unit_heads(mixed[:, :model_width], head_count).reshape(tokens_in.shape)
    key_part = unit_heads(mixed[:, model_width : 2 * model_width], head_count).reshape(
        tokens_in.shape
    )
    value_part = mixed[:, 2 * model_width :].astype(jnp.bfloat16).reshape(tokens_in.shape)
    return (queries, key_part, value_part)


def window_rows(tensor):
    groups, levels, lat_rows, lon_cells = tensor.shape[:4]
    shaped = tensor.reshape((groups, levels, lat_rows // WLAT, WLAT, lon_cells) + tensor.shape[4:])
    return jnp.moveaxis(shaped, 2, 0).reshape(
        (lat_rows // WLAT, groups * levels * WLAT * lon_cells) + tensor.shape[4:]
    )


def unwindow_rows(tensor, groups, levels, lon_cells):
    windows = tensor.shape[0]
    shaped = tensor.reshape((windows, groups, levels, WLAT, lon_cells) + tensor.shape[2:])
    return jnp.moveaxis(shaped, 0, 2).reshape(
        (groups, levels, windows * WLAT, lon_cells) + tensor.shape[2:]
    )


def region_windows(flag_rows, levels, lon_cells):
    lat_rows = flag_rows.shape[0]
    flag_grid = jnp.broadcast_to(flag_rows[None, :, None], (levels, lat_rows, lon_cells))
    shaped = flag_grid.reshape(levels, lat_rows // WLAT, WLAT, lon_cells)
    return jnp.moveaxis(shaped, 1, 0).reshape(lat_rows // WLAT, -1)


def bias_windows(key_bias):
    head_count, levels, lat_rows, lon_cells = key_bias.shape
    shaped = key_bias.reshape(head_count, levels, lat_rows // WLAT, WLAT, lon_cells)
    return jnp.transpose(shaped, (2, 0, 1, 3, 4)).reshape(lat_rows // WLAT, head_count, -1)


def window_terms(query_win, key_win, value_win, bias_win, query_reg, key_reg, scale):
    head_count = scale.shape[0]
    windows, queries, model_width = query_win.shape
    head_size = model_width // head_count
    key_count = key_win.shape[1]
    query_heads = query_win.reshape(windows, queries, head_count, head_size)
    key_heads = key_win.reshape(windows, key_count, head_count, head_size)
    value_heads = value_win.reshape(windows, key_count, head_count, head_size)
    scores = jnp.einsum(
        "wqhd,wkhd->whqk", query_heads, key_heads, preferred_element_type=jnp.float32
    )
    scores = scores * (scale / head_size)[None, :, None, None] + bias_win[:, :, None, :]
    same_region = query_reg[:, None, :, None] == key_reg[:, None, None, :]
    weights = jnp.where(same_region, jnp.exp(scores), 0.0).astype(jnp.bfloat16)
    totals = jnp.sum(weights.astype(jnp.float32), -1)
    weighted = jnp.einsum(
        "whqk,wkhd->wqhd", weights, value_heads, preferred_element_type=jnp.float32
    )
    return (weighted, totals)


def blocked_terms(query_win, key_win, value_win, bias_win, query_reg, key_reg, scale):
    windows, queries = query_win.shape[:2]
    pairing = 1

    def regroup(tensor):
        return tensor.reshape((windows // pairing, pairing) + tensor.shape[1:])

    def attend_block(block_args):
        return window_terms(
            block_args[0],
            block_args[1],
            block_args[2],
            block_args[3],
            block_args[4],
            block_args[5],
            scale,
        )

    weighted, totals = lax.map(
        attend_block,
        (
            regroup(query_win),
            regroup(key_win),
            regroup(value_win),
            regroup(bias_win),
            regroup(query_reg),
            regroup(key_reg),
        ),
    )
    return (
        weighted.reshape((windows,) + weighted.shape[2:]),
        totals.reshape((windows,) + totals.shape[2:]),
    )


def normalise(weighted, totals, groups, levels, lon_cells):
    ratio = weighted / jnp.transpose(totals, (0, 2, 1))[..., None]
    flat = ratio.astype(jnp.bfloat16).reshape(ratio.shape[0], ratio.shape[1], -1)
    return unwindow_rows(flat, groups, levels, lon_cells)


def project_out(attended, w_out):
    model_width = attended.shape[-1]
    projected = jnp.dot(
        attended.reshape(-1, model_width), w_out, preferred_element_type=jnp.float32
    )
    return projected.astype(jnp.bfloat16).reshape(attended.shape)


def per_device(fields, surface_mask, w_qkv, w_out, logit_scale, mask_bias, w_up, w_down):
    local_groups, levels, lat_rows, lon_cells, model_width = fields.shape
    head_count = logit_scale.shape[0]
    flag_marks = surface_mask.astype(jnp.bfloat16)
    lower_rows, lower_marks = passed_along(
        (fields[:, :, :SH_LAT], flag_marks[:, :SH_LAT]), "lat", -1
    )
    shifted = jnp.concatenate([fields[:, :, SH_LAT:], lower_rows], 2)
    marked = jnp.concatenate([flag_marks[:, SH_LAT:], lower_marks], 1)
    east_rows, east_marks = passed_along(
        (shifted[:, :, :, :SH_LON], marked[:, :, :SH_LON]), "lon", -1
    )
    rolled = jnp.concatenate([shifted[:, :, :, SH_LON:], east_rows], 3)
    rolled_marks = jnp.concatenate([marked[:, :, SH_LON:], east_marks], 2).astype(jnp.float32)
    key_bias = mask_bias[:, None, None, None] * rolled_marks[None]
    total_rows = lat_rows * lax.axis_size("lat")
    first_row = lax.axis_index("lat") * lat_rows
    gathered = lax.all_to_all(rolled, "grp", split_axis=2, concat_axis=0, tiled=True)
    part_rows = lat_rows // lax.axis_size("grp")
    offset = lax.axis_index("grp") * part_rows
    all_groups = gathered.shape[0]
    queries, key_part, value_part = project_heads(gathered, w_qkv, head_count)
    flag_rows = (
        first_row + offset + jnp.arange(part_rows, dtype=jnp.int32) >= total_rows - SH_LAT
    ).astype(jnp.int32)
    region_all = jnp.tile(region_windows(flag_rows, levels, lon_cells), (1, all_groups))
    bias_one = bias_windows(lax.dynamic_slice_in_dim(key_bias, offset, part_rows, 2))
    weighted, totals = blocked_terms(
        window_rows(queries),
        window_rows(key_part),
        window_rows(value_part),
        jnp.tile(bias_one, (1, 1, all_groups)),
        region_all,
        region_all,
        logit_scale,
    )
    attended = normalise(weighted, totals, all_groups, levels, lon_cells)
    projected = lax.all_to_all(
        project_out(attended, w_out), "grp", split_axis=0, concat_axis=2, tiled=True
    )
    west_rim = passed_along(projected[:, :, :, -SH_LON:], "lon", 1)
    unrolled = jnp.concatenate([west_rim, projected[:, :, :, :-SH_LON]], 3)
    north_rim = passed_along(unrolled[:, :, -SH_LAT:], "lat", 1)
    unrolled = jnp.concatenate([north_rim, unrolled[:, :, :-SH_LAT]], 2)
    residual = (fields.astype(jnp.float32) + unrolled.astype(jnp.float32)).astype(jnp.bfloat16)
    mlp_in = layer_norm(residual.astype(jnp.float32)).astype(jnp.bfloat16)
    hidden = jax.nn.gelu(
        jnp.dot(mlp_in.reshape(-1, model_width), w_up, preferred_element_type=jnp.float32),
        approximate=True,
    ).astype(jnp.bfloat16)
    update = jnp.dot(hidden, w_down, preferred_element_type=jnp.float32).reshape(fields.shape)
    return (residual.astype(jnp.float32) + update).astype(jnp.bfloat16)


def solution(mesh):
    return jax.shard_map(
        per_device,
        mesh=mesh,
        in_specs=(
            P("grp", None, "lat", "lon", None),
            P(None, "lat", "lon"),
            P(),
            P(),
            P(),
            P(),
            P(),
            P(),
        ),
        out_specs=P("grp", None, "lat", "lon", None),
        check_vma=False,
    )
```

profile of v0, /device:TPU:0, one launch (start us, length us, event | category | flops | bytes accessed | tf_op | source)
XLA Modules:
  0.0 152.2 jit_solution(5081694554470360105)
XLA Ops:
  0.0 0.9 convert_element_type.100
  0.9 5.1 %collective-permute-start.2 = (bf16[2,3,12]{2,0,1:T(2,128)(2,1)S(1)}, bf16[2,3,12]{2,0,1:T(2,128)(2,1)S(1)}, u32[]{:S(2)}, u32[]{:S(2)}) collective-permute-start(bf16[2,3,12]{2,0,1:T(2,128)(2,1)S(1)} %slice.67), channel_id=1, source_target_pairs={{0,3},{1,0},{2,1},{3,2},{4,7},{5,4},{6,5},{7,6},{8,11},{9,8},{10,9... | collective-permute-start | bytes 440 | tf_op jit(solution)/shard_map/ppermute | solution.py:13
  6.0 1.1 slice.47
  7.1 0.2 copy.49
  7.3 0.5 collective-permute-start
  7.8 1.5 %copy_dynamic-update-slice_fusion = bf16[3,2,12,12,512]{4,1,3,0,2:T(2,128)(2,1)S(1)} fusion(bf16[3,2,12,12,512]{4,1,3,2,0:T(2,128)(2,1)} %param.8), kind=kLoop, calls=%fused_computation.42 | loop fusion | bytes 1327104
  9.4 4.9 %collective-permute-done = bf16[3,2,3,12,512]{4,1,3,0,2:T(2,128)(2,1)S(1)} collective-permute-done((bf16[3,2,3,12,512]{4,1,3,0,2:T(2,128)(2,1)S(1)}, bf16[3,2,3,12,512]{4,1,3,0,2:T(2,128)(2,1)S(1)}, u32[]{:S(2)}, u32[]{:S(2)}) %collective-permute-start) | collective-permute-done | bytes 221216 | tf_op jit(solution)/shard_map/ppermute | solution.py:13
  14.2 0.2 constant_dynamic-update-slice_fusion
  14.4 1.4 fusion.28
  15.8 0.1 tile.14
  16.0 1.4 broadcast_compare_fusion
  17.4 0.1 slice_maximum_fusion
  17.5 1.6 %collective-permute-start.3 = (bf16[2,12,6]{2,0,1:T(2,128)(2,1)S(1)}, bf16[2,12,6]{2,0,1:T(2,128)(2,1)S(1)}, u32[]{:S(2)}, u32[]{:S(2)}) collective-permute-start(bf16[2,12,6]{2,0,1:T(2,128)(2,1)S(1)} %get-tuple-element.65), channel_id=1, source_target_pairs={{0,12},{4,0},{8,4},{12,8},{1,13},{5,1},{9,5},{13,9},{2,14},{6,2},{... | collective-permute-start | bytes 872 | tf_op jit(solution)/shard_map/ppermute | solution.py:13
  19.1 2.8 %collective-permute-done.1 = bf16[3,2,12,6,512]{4,1,3,0,2:T(2,128)(2,1)S(1)} collective-permute-done((bf16[3,2,12,6,512]{4,1,3,0,2:T(2,128)(2,1)}, bf16[3,2,12,6,512]{4,1,3,0,2:T(2,128)(2,1)S(1)}, u32[]{:S(2)}, u32[]{:S(2)}) %collective-permute-start.1) | collective-permute-done | bytes 442400 | tf_op jit(solution)/shard_map/ppermute | solution.py:13
  21.9 2.1 %pad_maximum_fusion.1 = bf16[3,2,12,12,512]{4,1,3,0,2:T(2,128)(2,1)} fusion(bf16[3,2,12,6,512]{4,1,3,0,2:T(2,128)(2,1)S(1)} %collective-permute-done.1, bf16[3,2,12,6,512]{4,1,3,0,2:T(2,128)(2,1)S(1)} %get-tuple-element.62), kind=kLoop, calls=%fused_computation.39 | loop fusion | flops 442368 | bytes 1769472 | tf_op jit(solution)/shard_map/concatenate | solution.py:150
  24.0 3.6 %all-to-all-start = ((bf16[3,2,12,12,512]{4,1,3,0,2:T(2,128)(2,1)}), bf16[3,2,12,12,512]{4,1,3,0,2:T(2,128)(2,1)S(1)}, u32[]{:S(2)}, u32[]{:S(2)}) async-start(bf16[3,2,12,12,512]{4,1,3,0,2:T(2,128)(2,1)} %pad_maximum_fusion.1), calls=%async_computation | async-start | bytes 1769472 | tf_op jit(solution)/shard_map/all_to_all | solution.py:155
  27.7 0.1 tile.16
  27.8 0.1 add.97
  27.9 12.1 %all-to-all-done = bf16[3,2,12,12,512]{4,1,3,0,2:T(2,128)(2,1)S(1)} async-done(((bf16[3,2,12,12,512]{4,1,3,0,2:T(2,128)(2,1)}), bf16[3,2,12,12,512]{4,1,3,0,2:T(2,128)(2,1)S(1)}, u32[]{:S(2)}, u32[]{:S(2)}) %all-to-all-start) | async-done | bytes 884768 | tf_op jit(solution)/shard_map/all_to_all | solution.py:155
  40.0 1.0 convert.9
  41.0 0.4 fusion.22
  41.4 0.6 multiply_reduce_fusion
  42.0 0.1 div.40
  42.1 1.7 %copy.58 = f32[3,2,2,6,12,512]{5,4,3,1,0,2:T(8,128)} copy(bf16[3,2,2,6,12,512]{5,1,4,0,3,2:T(2,128)(2,1)S(1)} %bitcast.49) | data formatting | bytes 2654208 | tf_op jit(solution)/shard_map/convert_element_type | solution.py:29
  43.9 0.1 rsqrt.36
  44.0 2.8 %reshape.243 = f32[864,512]{1,0:T(8,128)} reshape(f32[2,3,2,6,12,512]{5,4,3,2,1,0:T(8,128)} %bitcast.47) | data formatting | bytes 3538944 | tf_op jit(solution)/shard_map/convert_element_type | solution.py:29
  46.8 3.5 %fusion.19 = f32[864,1536]{1,0:T(8,128)S(1)} fusion(bf16[512,1536]{1,0:T(8,128)(2,1)} %param.10, f32[864,512]{1,0:T(8,128)} %reshape.243, f32[864]{0:T(1024)S(1)} %rsqrt.36, f32[864]{0:T(1024)S(1)} %div.40), kind=kOutput, calls=%fused_computation.38 | convolution fusion | flops 1360281600 | bytes 8657664 | tf_op jit(solution)/shard_map/dot_general | solution.py:30
  50.4 1.1 slice.79
  51.5 1.4 copy-done.1
  52.9 2.2 %slice_multiply_fusion = (f32[864,512]{1,0:T(8,128)}, f32[864,512]{1,0:T(8,128)}) fusion(f32[864,1536]{1,0:T(8,128)S(1)} %fusion.19), kind=kLoop, calls=%fused_computation.32 | loop fusion | flops 884736 | bytes 7077888 | tf_op jit(solution)/shard_map/mul | solution.py:23
  55.2 1.5 %copy.33 = bf16[864,512]{0,1:T(8,128)(2,1)S(1)} copy(bf16[864,512]{1,0:T(8,128)(2,1)} %slice.79) | data formatting | bytes 1769472 | tf_op jit(solution)/shard_map/slice | solution.py:35
  56.7 2.7 %copy.37 = f32[864,512]{0,1:T(8,128)} copy(f32[864,512]{1,0:T(8,128)} %get-tuple-element.58) | data formatting | bytes 3538944 | tf_op jit(solution)/shard_map/mul | solution.py:23
  59.5 1.6 %bitcast_reduce_fusion = f32[864,8]{0,1:T(8,128)S(1)} fusion(f32[864,512]{0,1:T(8,128)} %copy.37), kind=kLoop, calls=%fused_computation.26 | loop fusion | flops 435456 | bytes 1797120 | tf_op jit(solution)/shard_map/reduce_sum | solution.py:23
  61.1 1.4 mul.124
  62.5 2.8 %copy.38 = f32[864,512]{1,0:T(8,128)} copy(f32[864,512]{0,1:T(8,128)} %bitcast.50) | data formatting | bytes 3538944 | tf_op jit(solution)/shard_map/mul | solution.py:23
  65.3 2.7 %copy.34 = f32[864,512]{0,1:T(8,128)} copy(f32[864,512]{1,0:T(8,128)} %get-tuple-element.59) | data formatting | bytes 3538944 | tf_op jit(solution)/shard_map/mul | solution.py:23
  68.1 1.6 %bitcast_reduce_fusion.1 = f32[864,8]{0,1:T(8,128)S(1)} fusion(f32[864,512]{0,1:T(8,128)} %copy.34), kind=kLoop, calls=%fused_computation.27 | loop fusion | flops 435456 | bytes 1797120 | tf_op jit(solution)/shard_map/reduce_sum | solution.py:23
  69.7 1.4 mul.119
  71.1 2.7 %copy.35 = f32[864,512]{1,0:T(8,128)} copy(f32[864,512]{0,1:T(8,128)} %bitcast.51) | data formatting | bytes 3538944 | tf_op jit(solution)/shard_map/mul | solution.py:23
  73.9 4.9 %multiply_convert_fusion = (bf16[864,512]{1,0:T(8,128)(2,1)}, bf16[864,512]{1,0:T(8,128)(2,1)}) fusion(f32[864,512]{1,0:T(8,128)} %copy.38, f32[864,1536]{1,0:T(8,128)} %copy-done.1, f32[864,512]{1,0:T(8,128)} %copy.35), kind=kLoop, calls=%fused_computation.29 | loop fusion | flops 1769472 | bytes 8847360 | tf_op jit(solution)/shard_map/convert_element_type | solution.py:24
  78.8 2.2 %copy.39 = bf16[864,512]{0,1:T(8,128)(2,1)} copy(bf16[864,512]{1,0:T(8,128)(2,1)} %get-tuple-element.56) | data formatting | bytes 1769472 | tf_op jit(solution)/shard_map/convert_element_type | solution.py:24
  81.0 2.2 %copy.36 = bf16[864,512]{0,1:T(8,128)(2,1)} copy(bf16[864,512]{1,0:T(8,128)(2,1)} %get-tuple-element.57) | data formatting | bytes 1769472 | tf_op jit(solution)/shard_map/convert_element_type | solution.py:24
  83.2 9.4 %convert_reduce_fusion = (f32[8,864]{1,0:T(8,128)S(1)}, bf16[8,864,864]{1,2,0:T(8,128)(2,1)S(1)}) fusion(f32[8,864]{1,0:T(8,128)S(1)} %add.97, f32[8]{0:T(128)S(1)} %broadcast_multiply_fusion.3, bf16[864,8,64]{0,2,1:T(8,128)(2,1)} %bitcast.56, bf16[864,8,64]{0,2,1:T(8,128)(2,1)} %bitcast.55, pred[864,864]{0,1:T(8,128)(4,1)} %broadcast_compare_fusion), kind=kOutput, calls=%fused_computation | convolution fusion | flops 800236800 | bytes 14515232 | tf_op jit(solution)/shard_map/while/body/eval_jaxpr/wqhd,wkhd->whqk/dot_general | solution.py:76
  92.6 2.2 %fusion.29 = f32[8,64,864]{2,1,0:T(8,128)S(1)} fusion(bf16[864,8,64]{0,2,1:T(8,128)(2,1)S(1)} %bitcast.53, bf16[8,864,864]{1,2,0:T(8,128)(2,1)S(1)} %get-tuple-element.67), kind=kOutput, calls=%fused_computation.65 | convolution fusion | flops 764411904 | bytes 14598144 | tf_op jit(solution)/shard_map/while/body/eval_jaxpr/whqk,wkhd->wqhd/dot_general | solution.py:83
  94.9 0.1 fusion.17
  95.0 0.9 copy-done.4
  95.9 1.6 %convolution_convert_fusion = bf16[864,512]{1,0:T(8,128)(2,1)} fusion(bf16[864,512]{0,1:T(8,128)(2,1)S(1)} %fusion.17, bf16[512,512]{1,0:T(8,128)(2,1)S(1)} %copy-done.4), kind=kOutput, calls=%fused_computation.35 | convolution fusion | flops 453427200 | bytes 2293760 | tf_op jit(solution)/shard_map/dot_general | solution.py:132
  97.5 1.5 reshape.240
  99.0 0.9 copy.42
  99.9 15.2 %all_to_all.27 = bf16[6,2,6,12,512]{4,1,3,2,0:T(2,128)(2,1)S(1)} all-to-all(bf16[6,2,6,12,512]{4,1,3,2,0:T(2,128)(2,1)S(1)} %copy.42), channel_id=1, replica_groups=mesh['grp'=2,'lon'=4,'lat'=4] {'grp'}, dimensions={0} | all-to-all | bytes 1769472 | tf_op jit(solution)/shard_map/all_to_all | solution.py:175
  115.1 0.2 copy.43
  115.4 0.2 fusion.27
  115.6 0.5 copy.44
  116.1 7.7 %collective-permute-done.4 = bf16[3,2,12,6,512]{4,1,3,2,0:T(2,128)(2,1)S(1)} collective-permute-done((bf16[3,2,12,6,512]{4,1,3,2,0:T(2,128)(2,1)S(1)}, bf16[3,2,12,6,512]{4,1,3,2,0:T(2,128)(2,1)S(1)}, u32[]{:S(2)}, u32[]{:S(2)}) %collective-permute-start.4) | collective-permute-done | bytes 442400 | tf_op jit(solution)/shard_map/ppermute | solution.py:13
  123.9 0.1 pad_maximum_fusion.2
  124.1 9.6 %collective-permute-done.5 = bf16[3,2,3,12,512]{4,3,2,1,0:T(8,128)(2,1)S(1)} collective-permute-done((bf16[3,2,3,12,512]{4,3,2,1,0:T(8,128)(2,1)S(1)}, bf16[3,2,3,12,512]{4,3,2,1,0:T(8,128)(2,1)S(1)}, u32[]{:S(2)}, u32[]{:S(2)}) %collective-permute-start.5) | collective-permute-done | bytes 221216 | tf_op jit(solution)/shard_map/ppermute | solution.py:13
  133.7 0.6 convert_reduce_fusion.1
  134.3 0.6 fusion.12
  134.9 1.4 fusion.13
  136.3 2.1 %reshape.241 = bf16[864,512]{1,0:T(8,128)(2,1)} reshape(bf16[3,2,12,12,512]{4,3,2,1,0:T(8,128)(2,1)} %fusion.13) | data formatting | bytes 1769472 | tf_op jit(solution)/shard_map/reshape | solution.py:185
  138.4 7.1 %fusion.8 = f32[864,512]{1,0:T(8,128)} fusion(bf16[2048,512]{1,0:T(8,128)(2,1)S(1)} %copy-done, bf16[864,512]{1,0:T(8,128)(2,1)} %reshape.241, bf16[512,2048]{1,0:T(8,128)(2,1)} %param.14), kind=kOutput, calls=%fused_computation.11 | convolution fusion | flops 3639803904 | bytes 6848512 | tf_op jit(solution)/shard_map/dot_general | solution.py:188
  145.5 2.7 %reshape.242 = f32[3,2,12,12,512]{4,3,2,1,0:T(8,128)} reshape(f32[864,512]{1,0:T(8,128)} %fusion.8) | data formatting | bytes 3538944 | tf_op jit(solution)/shard_map/reshape | solution.py:188
  148.2 2.1 %fusion.14 = bf16[3,2,12,12,512]{4,3,2,1,0:T(8,128)(2,1)S(1)} fusion(f32[3,2,12,12,512]{4,3,2,1,0:T(8,128)} %reshape.242, bf16[3,2,12,12,512]{4,3,2,1,0:T(8,128)(2,1)S(1)} %get-tuple-element.55), kind=kLoop, calls=%fused_computation.19 | loop fusion | flops 1327104 | bytes 3538944 | tf_op jit(solution)/shard_map/convert_element_type | solution.py:189
  150.3 1.8 %copy.46 = bf16[3,2,12,12,512]{4,1,3,2,0:T(2,128)(2,1)} copy(bf16[3,2,12,12,512]{4,3,2,1,0:T(8,128)(2,1)S(1)} %fusion.14) | data formatting | bytes 1769472 | tf_op jit(solution)/shard_map/convert_element_type | solution.py:189
  (34 shorter events, 0.6 us)
Async XLA Ops:
  0.0 138.4 %copy-start = (bf16[2048,512]{1,0:T(8,128)(2,1)S(1)}, bf16[2048,512]{1,0:T(8,128)(2,1)}, u32[]{:S(2)}) copy-start(bf16[2048,512]{1,0:T(8,128)(2,1)} %param.15) | copy-start | bytes 6291460
  0.0 9.3 %copy-start.5 = (f32[8]{0:T(128)S(1)}, f32[8]{0:T(128)}, u32[]{:S(2)}) copy-start(f32[8]{0:T(128)} %param.12) | copy-start | bytes 100
  0.9 16.5 %collective-permute-start.2 = (bf16[2,3,12]{2,0,1:T(2,128)(2,1)S(1)}, bf16[2,3,12]{2,0,1:T(2,128)(2,1)S(1)}, u32[]{:S(2)}, u32[]{:S(2)}) collective-permute-start(bf16[2,3,12]{2,0,1:T(2,128)(2,1)S(1)} %slice.67), channel_id=1, source_target_pairs={{0,3},{1,0},{2,1},{3,2},{4,7},{5,4},{6,5},{7,6},{8,11},{9,8},{10,9... | collective-permute-start | bytes 440 | tf_op jit(solution)/shard_map/ppermute | solution.py:13
  7.3 6.9 %collective-permute-start = (bf16[3,2,3,12,512]{4,1,3,0,2:T(2,128)(2,1)S(1)}, bf16[3,2,3,12,512]{4,1,3,0,2:T(2,128)(2,1)S(1)}, u32[]{:S(2)}, u32[]{:S(2)}) collective-permute-start(bf16[3,2,3,12,512]{4,1,3,0,2:T(2,128)(2,1)S(1)} %copy.49), channel_id=1, source_target_pairs={{0,3},{1,0},{2,1},{3,2},{4,7},{5,4},{6,5},{7,6},{8,11},{9,8},{10,9... | collective-permute-start | bytes 663560 | tf_op jit(solution)/shard_map/ppermute | solution.py:13
  15.8 6.1 %collective-permute-start.1 = (bf16[3,2,12,6,512]{4,1,3,0,2:T(2,128)(2,1)}, bf16[3,2,12,6,512]{4,1,3,0,2:T(2,128)(2,1)S(1)}, u32[]{:S(2)}, u32[]{:S(2)}) collective-permute-start(bf16[3,2,12,6,512]{4,1,3,0,2:T(2,128)(2,1)} %get-tuple-element.63), channel_id=1, source_target_pairs={{0,12},{4,0},{8,4},{12,8},{1,13},{5,1},{9,5},{13,9},{2,14},{6,2},{... | collective-permute-start | bytes 1327112 | tf_op jit(solution)/shard_map/ppermute | solution.py:13
  16.0 11.6 %copy-start.3 = (f32[8]{0:T(128)S(1)}, f32[8]{0:T(128)}, u32[]{:S(2)}) copy-start(f32[8]{0:T(128)} %param.13) | copy-start | bytes 100
  17.5 10.0 %collective-permute-start.3 = (bf16[2,12,6]{2,0,1:T(2,128)(2,1)S(1)}, bf16[2,12,6]{2,0,1:T(2,128)(2,1)S(1)}, u32[]{:S(2)}, u32[]{:S(2)}) collective-permute-start(bf16[2,12,6]{2,0,1:T(2,128)(2,1)S(1)} %get-tuple-element.65), channel_id=1, source_target_pairs={{0,12},{4,0},{8,4},{12,8},{1,13},{5,1},{9,5},{13,9},{2,14},{6,2},{... | collective-permute-start | bytes 872 | tf_op jit(solution)/shard_map/ppermute | solution.py:13
  24.0 16.1 %all-to-all-start = ((bf16[3,2,12,12,512]{4,1,3,0,2:T(2,128)(2,1)}), bf16[3,2,12,12,512]{4,1,3,0,2:T(2,128)(2,1)S(1)}, u32[]{:S(2)}, u32[]{:S(2)}) async-start(bf16[3,2,12,12,512]{4,1,3,0,2:T(2,128)(2,1)} %pad_maximum_fusion.1), calls=%async_computation | async-start | bytes 1769472 | tf_op jit(solution)/shard_map/all_to_all | solution.py:155
  50.4 2.6 %copy-start.1 = (f32[864,1536]{1,0:T(8,128)}, f32[864,1536]{1,0:T(8,128)S(1)}, u32[]{:S(2)}) copy-start(f32[864,1536]{1,0:T(8,128)S(1)} %fusion.19) | copy-start | bytes 15925252
  94.9 1.0 copy-start.4
  115.6 18.1 %copy-start.2 = (bf16[3,2,12,12,512]{4,1,3,2,0:T(2,128)(2,1)S(1)}, bf16[3,2,12,12,512]{4,1,3,2,0:T(2,128)(2,1)}, u32[]{:S(2)}) copy-start(bf16[3,2,12,12,512]{4,1,3,2,0:T(2,128)(2,1)} %param.8) | copy-start | bytes 2654212
  116.1 7.8 %collective-permute-start.4 = (bf16[3,2,12,6,512]{4,1,3,2,0:T(2,128)(2,1)S(1)}, bf16[3,2,12,6,512]{4,1,3,2,0:T(2,128)(2,1)S(1)}, u32[]{:S(2)}, u32[]{:S(2)}) collective-permute-start(bf16[3,2,12,6,512]{4,1,3,2,0:T(2,128)(2,1)S(1)} %copy.44), channel_id=1, source_target_pairs={{0,4},{4,8},{8,12},{12,0},{1,5},{5,9},{9,13},{13,1},{2,6},{6,10},{... | collective-permute-start | bytes 1327112 | tf_op jit(solution)/shard_map/ppermute | solution.py:13
  124.0 9.6 %collective-permute-start.5 = (bf16[3,2,3,12,512]{4,3,2,1,0:T(8,128)(2,1)S(1)}, bf16[3,2,3,12,512]{4,3,2,1,0:T(8,128)(2,1)S(1)}, u32[]{:S(2)}, u32[]{:S(2)}) collective-permute-start(bf16[3,2,3,12,512]{4,3,2,1,0:T(8,128)(2,1)S(1)} %pad_maximum_fusion.2), channel_id=1, source_target_pairs={{0,1},{1,2},{2,3},{3,0},{4,5},{5,6},{6,7},{7,4},{8,9},{9,10},{10,1... | collective-permute-start | bytes 663560 | tf_op jit(solution)/shard_map/ppermute | solution.py:13
where the time goes:
time: 153 us; the launch traced here: 152 us
  local copies, waits for them, and re-layouts  42.8 us (28%)
  waiting for transfers between devices  37 us (24%)
  matrix products  23.8 us (16%)
  other arithmetic  22 us (14%)
  blocking collectives  15.2 us (10%)
  starting transfers between devices  10.9 us (7%)
    ppermute x6, waiting for transfers between devices, passed_along(): lax.ppermute(array, axis, [(i, (i + by) % count) for i in range(count)])  24.9 us
    all_to_all x1, blocking collectives, per_device(): lax.all_to_all(project_out(attended, w_out), 'grp', split_axis=0, concat_...  15.2 us
    all_to_all x1, waiting for transfers between devices, per_device(): lax.all_to_all(rolled, 'grp', split_axis=2, concat_axis=0, tiled=True)  12.1 us
    dot_general x1, matrix products, window_terms(): jnp.einsum('wqhd,wkhd->whqk', query_heads, key_heads, preferred_element_t...  9.39 us
    mul x4, local copies, waits for them, and re-layouts, unit_heads(): shaped * lax.rsqrt(jnp.mean(shaped * shaped, -1, keepdims=True) + 1e-06)  8.33 us
    ppermute x6, starting transfers between devices, passed_along(): lax.ppermute(array, axis, [(i, (i + by) % count) for i in range(count)])  7.39 us
    dot_general x1, matrix products, per_device(): jnp.dot(hidden, w_down, preferred_element_type=jnp.float32)  7.14 us
    mul x2, local copies, waits for them, and re-layouts, unit_heads(): shaped * shaped  5.49 us
  transfers between devices with their start and end apart: 7, of which 5 were waited for; matrix products, arithmetic and copies ran while one was open for 6% of the time, Pallas kernels for 0%

commit v1 on v0

v1 whole, which is shorter than its diff:
```python
import functools
import math

import jax
import jax.numpy as jnp
from jax import lax
from jax.experimental import pallas as pl
from jax.experimental.pallas import tpu as pltpu
from jax.sharding import PartitionSpec as P

SH_LAT = 3
SH_LON = 6
LOG2E = math.log2(math.e)
FAR = -30000.0
MESH = pl.DeviceIdType.MESH
BF16 = jnp.bfloat16
F32 = jnp.float32


def layer_norm(values):
    centred = values - jnp.mean(values, -1, keepdims=True)
    return centred * lax.rsqrt(jnp.mean(centred * centred, -1, keepdims=True) + 1e-05)


def iota(shape, axis):
    return lax.broadcasted_iota(jnp.int32, shape, axis)


def dot(left, right):
    return jnp.dot(left, right, preferred_element_type=F32)


def dot_t(left, right):
    return lax.dot_general(left, right, (((1,), (1,)), ((), ())), preferred_element_type=F32)


def kernel(
    real, heads,
    x_ref, qscale_ref, bias_ref, wqkv_hbm, wout_hbm, wup_hbm, wdown_hbm,
    out_ref,
    wqkv, wout, wup, wdown, win, ret, proj, att, qs, ks, vs, kx,
    wsem, send1, recv1, send2, recv2,
):
    rows, width = x_ref.shape[2:]
    pair_rows = 2 * rows
    half = 2 * pair_rows
    total = 2 * half
    pairs = heads // 2
    head_size = width // heads
    lanes = 2 * head_size

    g, a, b = lax.axis_index("grp"), lax.axis_index("lat"), lax.axis_index("lon")
    na, nb = lax.axis_size("lat"), lax.axis_size("lon")

    weights = [
        pltpu.make_async_copy(src, dst, wsem.at[i])
        for i, (src, dst) in enumerate(
            ((wqkv_hbm, wqkv), (wout_hbm, wout), (wup_hbm, wup), (wdown_hbm, wdown))
        )
    ]
    for copy in weights:
        copy.start()

    barrier = pltpu.get_barrier_semaphore()
    greeted = 0
    for d in (0, 1):
        for da in (-1, 0, 1):
            for db in (-1, 0, 1):
                if d or da or db:
                    pl.semaphore_signal(
                        barrier,
                        inc=1,
                        device_id={
                            "grp": (g + d) % 2,
                            "lat": (a + da + na) % na,
                            "lon": (b + db + nb) % nb,
                        },
                        device_id_type=MESH,
                    )
                    greeted += 1
    pl.semaphore_wait(barrier, greeted)

    def parity_to(d, cc):
        return (g + d + b + cc) % 2

    def row_of(parity, rr):
        return (1 + 2 * parity + rr) % 4

    def forward(d, cc, rr, act):
        parity = parity_to(d, cc)
        r = row_of(parity, rr)
        p = 2 * d + cc
        src = x_ref.at[r, 1 - cc]
        dst = win.at[p, rr]
        i = 2 * p + rr
        edge = rr * parity

        def local():
            return pltpu.make_async_copy(src, dst, recv1.at[i])

        def remote():
            return pltpu.make_async_remote_copy(
                src_ref=src, dst_ref=dst, send_sem=send1.at[i], recv_sem=recv1.at[i],
                device_id={
                    "grp": (g + d) % 2,
                    "lat": (a - edge + na) % na,
                    "lon": (b - cc + nb) % nb,
                },
                device_id_type=MESH,
            )

        act(d, cc, rr, parity, local, remote)

    def backward(d, cc, rr, act):
        parity = (g + b) % 2
        p = 2 * d + cc
        src = proj.at[p, rr]
        dst = ret.at[p, rr]
        i = 2 * p + rr
        edge = rr * parity

        def local():
            return pltpu.make_async_copy(src, dst, recv2.at[i])

        def remote():
            return pltpu.make_async_remote_copy(
                src_ref=src, dst_ref=dst, send_sem=send2.at[i], recv_sem=recv2.at[i],
                device_id={
                    "grp": (g + d) % 2,
                    "lat": (a + edge) % na,
                    "lon": (b + cc) % nb,
                },
                device_id_type=MESH,
            )

        act(d, cc, rr, parity, local, remote)

    def start(d, cc, rr, parity, local, remote):
        if d or cc:
            remote().start()
        elif rr == 0:
            local().start()
        else:
            pl.when(parity == 0)(lambda: local().start())
            pl.when(parity == 1)(lambda: remote().start())

    def finish(d, cc, rr, parity, local, remote):
        if d or cc:
            remote().wait_send()
        elif rr == 1:
            pl.when(parity == 1)(lambda: remote().wait_send())

    for d, cc in ((1, 0), (1, 1), (0, 1), (0, 0)):
        for rr in (1, 0):
            forward(d, cc, rr, start)

    last = jnp.where(a == na - 1, (g + b) % 2, 0)
    row_in_block = iota((pair_rows, lanes), 0) % rows
    valid = row_in_block < real
    lane = iota((pair_rows, lanes), 1)
    late = jnp.where(iota((pair_rows, lanes), 0) >= rows, last, 0)
    raw_bias = bias_ref[...]
    bias_hi = raw_bias.astype(BF16).astype(F32)
    bias_row = jnp.where(iota(raw_bias.shape, 1) % 2 == 0, bias_hi, raw_bias - bias_hi)
    far = jnp.where(
        lane == 2 * heads, FAR * late.astype(F32),
        jnp.where(lane == 2 * heads + 1, FAR * (1 - late).astype(F32), 0.0),
    )
    span = 2 * lanes
    blocks = jnp.where(
        iota((span, span), 0) // head_size == iota((span, span), 1) // head_size,
        1.0 / head_size, 0.0,
    ).astype(BF16)
    eye = jnp.where(iota((rows, lanes), 0) == iota((rows, lanes), 1), 1.0, 0.0).astype(BF16)
    ones = jnp.where(valid, 1.0, 0.0).astype(BF16)

    weights[0].wait()

    def project(p, carry):
        for rr in (0, 1):
            pltpu.make_async_copy(win.at[p, rr], win.at[p, rr], recv1.at[2 * p + rr]).wait()
        both = win[p].reshape(pair_rows, width)
        normed = layer_norm(both.astype(F32)).astype(BF16)
        here = pl.ds(p * pair_rows, pair_rows)
        for part, store in ((0, qs), (1, ks)):
            for s in range(width // span):
                lo = s * span
                mixed = dot(normed, wqkv[:, part * width + lo : part * width + lo + span])
                square = dot((mixed * mixed).astype(BF16), blocks)
                unit = mixed * lax.rsqrt(square + 1e-06)
                if part == 0:
                    unit = unit * qscale_ref[:, lo : lo + span]
                unit = unit.astype(BF16)
                store[2 * s, here] = unit[:, :lanes]
                store[2 * s + 1, here] = unit[:, lanes:]
        for s in range(width // span):
            lo = 2 * width + s * span
            mixed = dot(normed, wqkv[:, lo : lo + span])
            for k in (0, 1):
                vs[2 * s + k, here] = jnp.where(
                    valid, mixed[:, k * lanes : (k + 1) * lanes], 0.0
                ).astype(BF16)
        marks = jnp.concatenate(
            [
                dot_t(eye, jnp.broadcast_to(win[p, rr, real : real + 1, :lanes], (lanes, lanes)))
                for rr in (0, 1)
            ],
            0,
        )
        kx[here] = (marks * bias_row + far).astype(BF16)
        return carry

    lax.fori_loop(0, 4, project, 0)
    weights[1].wait()

    q_lane = iota((half, lanes), 1)
    q_late = jnp.where((iota((half, lanes), 0) // rows) % 2 == 1, last, 0)
    q_region = jnp.where(
        q_lane == 2 * heads, (1 - q_late).astype(F32),
        jnp.where(q_lane == 2 * heads + 1, q_late.astype(F32), 0.0),
    )
    low = q_lane < head_size
    ones_all = jnp.concatenate([ones] * (total // pair_rows), 0)

    for d in (1, 0):

        def attend(pair, carry):
            query = qs[pair, d * half : (d + 1) * half]
            keys = jnp.concatenate([ks[pair], kx[...]], 1)
            values = jnp.concatenate([vs[pair], ones_all], 1)
            ratios = []
            for e in (0, 1):
                chosen = jnp.where(low if e == 0 else ~low, query.astype(F32), 0.0).astype(BF16)
                extra = jnp.where(q_lane // 2 == 2 * pair + e, 1.0, q_region).astype(BF16)
                scores = dot_t(jnp.concatenate([chosen, extra], 1), keys)
                summed = dot(jnp.exp2(scores).astype(BF16), values)
                ratios.append(summed[:, :lanes] / summed[:, lanes:])
            att[:, pl.ds(pl.multiple_of(pair * lanes, lanes), lanes)] = jnp.where(
                low, ratios[0], ratios[1]
            ).astype(BF16)
            return carry

        lax.fori_loop(0, pairs, attend, 0)
        projected = dot(att[...], wout[...]).astype(BF16)
        proj[2 * d : 2 * d + 2] = projected.reshape(2, 2, rows, width)
        for cc in (1, 0):
            for rr in (1, 0):
                backward(d, cc, rr, start)

    weights[2].wait()
    weights[3].wait()

    def join(p, carry):
        for rr in (0, 1):
            pltpu.make_async_copy(ret.at[p, rr], ret.at[p, rr], recv2.at[2 * p + rr]).wait()
        d, cc = p // 2, p % 2
        parity = parity_to(d, cc)
        r0, r1 = row_of(parity, 0), row_of(parity, 1)
        own = jnp.concatenate([x_ref[r0, 1 - cc], x_ref[r1, 1 - cc]], 0)
        back = ret[p].reshape(pair_rows, width)
        residual = (own.astype(F32) + back.astype(F32)).astype(BF16).astype(F32)
        mlp_in = layer_norm(residual).astype(BF16)
        joined = residual
        hidden_size = wup.shape[1]
        piece = 512
        for s in range(hidden_size // piece):
            up = dot(mlp_in, wup[:, s * piece : (s + 1) * piece])
            inner = math.sqrt(2.0 / math.pi) * (up + 0.044715 * (up * up * up))
            hidden = (0.5 * up * (1.0 + jnp.tanh(inner))).astype(BF16)
            joined = joined + dot(hidden, wdown[s * piece : (s + 1) * piece, :])
        joined = joined.astype(BF16)
        out_ref[r0, 1 - cc] = joined[:rows]
        out_ref[r1, 1 - cc] = joined[rows:]
        return carry

    lax.fori_loop(0, 4, join, 0)

    for d in (0, 1):
        for cc in (0, 1):
            for rr in (0, 1):
                forward(d, cc, rr, finish)
                backward(d, cc, rr, finish)


def per_device(fields, surface_mask, w_qkv, w_out, logit_scale, mask_bias, w_up, w_down):
    groups, levels, nlat, nlon, width = fields.shape
    heads = logit_scale.shape[0]
    head_size = width // heads
    hidden_size = w_up.shape[1]
    tris, sides = nlat // SH_LAT, nlon // SH_LON
    real = groups * levels * SH_LAT * SH_LON
    rows = -(-(real + 1) // 16) * 16
    total = 8 * rows

    split = fields.reshape(groups, levels, tris, SH_LAT, sides, SH_LON, width)
    tokens = jnp.transpose(split, (2, 4, 0, 1, 3, 5, 6)).reshape(tris, sides, real, width)
    flags = surface_mask.reshape(levels, tris, SH_LAT, sides, SH_LON)
    flags = jnp.transpose(flags, (1, 3, 0, 2, 4)).reshape(tris, sides, 1, real // groups)
    flags = jnp.tile(flags.astype(BF16), (1, 1, 1, groups))
    flags = jnp.pad(flags, ((0, 0), (0, 0), (0, rows - real - 1), (0, width - real)))
    x = jnp.concatenate([tokens, flags], 2)

    qscale = jnp.repeat(logit_scale * (LOG2E / head_size), head_size)[None]
    bias = jnp.pad(jnp.repeat(mask_bias * LOG2E, 2), (0, 2 * head_size - 2 * heads))[None]

    vmem = pl.BlockSpec(memory_space=pltpu.VMEM)
    anywhere = pl.BlockSpec(memory_space=pl.ANY)
    joined = pl.pallas_call(
        functools.partial(kernel, real, heads),
        out_shape=jax.ShapeDtypeStruct(x.shape, BF16),
        in_specs=[vmem] * 3 + [anywhere] * 4,
        out_specs=vmem,
        scratch_shapes=[
            pltpu.VMEM(w_qkv.shape, BF16),
            pltpu.VMEM(w_out.shape, BF16),
            pltpu.VMEM(w_up.shape, BF16),
            pltpu.VMEM(w_down.shape, BF16),
            pltpu.VMEM((4, 2, rows, width), BF16),
            pltpu.VMEM((4, 2, rows, width), BF16),
            pltpu.VMEM((4, 2, rows, width), BF16),
            pltpu.VMEM((total // 2, width), BF16),
            pltpu.VMEM((heads // 2, total, 2 * head_size), BF16),
            pltpu.VMEM((heads // 2, total, 2 * head_size), BF16),
            pltpu.VMEM((heads // 2, total, 2 * head_size), BF16),
            pltpu.VMEM((total, 2 * head_size), BF16),
            pltpu.SemaphoreType.DMA((4,)),
            pltpu.SemaphoreType.DMA((8,)),
            pltpu.SemaphoreType.DMA((8,)),
            pltpu.SemaphoreType.DMA((8,)),
            pltpu.SemaphoreType.DMA((8,)),
        ],
        compiler_params=pltpu.CompilerParams(
            collective_id=0, has_side_effects=True, vmem_limit_bytes=56 * 1024 * 1024
        ),
        name="window_block",
    )(x, qscale, bias, w_qkv, w_out, w_up, w_down)

    kept = joined[:, :, :real].reshape(tris, sides, groups, levels, SH_LAT, SH_LON, width)
    return jnp.transpose(kept, (2, 3, 0, 4, 1, 5, 6)).reshape(fields.shape)


def solution(mesh):
    return jax.shard_map(
        per_device,
        mesh=mesh,
        in_specs=(
            P("grp", None, "lat", "lon", None),
            P(None, "lat", "lon"),
            P(),
            P(),
            P(),
            P(),
            P(),
            P(),
        ),
        out_specs=P("grp", None, "lat", "lon", None),
        check_vma=False,
    )
```

time: 153 us -> 55 us (0.36)
  the two profiles are of different devices: /device:TPU:0 before, /device:TPU:1 now
where the time goes in v1:
time: 55 us; the launch traced here: 54.8 us
  Pallas kernels  46.2 us (84%)
  local copies, waits for them, and re-layouts  7.49 us (14%)
  other arithmetic  1.03 us (2%)
    pallas_call x1, Pallas kernels, per_device(): pl.pallas_call(functools.partial(kernel, real, heads), out_shape=jax.Shap...  46.2 us
    slice x1, local copies, waits for them, and re-layouts, per_device(): joined[:, :, :real]  2.09 us
    reshape x1, local copies, waits for them, and re-layouts, per_device(): split = fields.reshape(groups, levels, tris, SH_LAT, sides, SH_LON, width)  1.86 us
    transpose x1, local copies, waits for them, and re-layouts, per_device(): return jnp.transpose(kept, (2, 3, 0, 4, 1, 5, 6)).reshape(fields.shape)  1.64 us

profile of v1, /device:TPU:1, one launch (start us, length us, event | category | flops | bytes accessed | tf_op | source)
XLA Modules:
  0.0 54.8 jit_solution(2194389243781589021)
XLA Ops:
  0.0 0.0 copy-start
  0.0 1.9 %copy.16 = bf16[3,2,4,3,2,6,512]{6,4,5,3,1,0,2:T(2,128)(2,1)S(1)} copy(bf16[3,2,4,3,2,6,512]{6,1,5,4,3,2,0:T(2,128)(2,1)} %bitcast.19) | data formatting | bytes 1769472 | tf_op jit(solution)/shard_map/reshape | solution.py:295
  1.9 0.0 copy-start.1
  1.9 0.0 copy-start.2
  1.9 0.1 copy.19
  2.0 0.0 copy-done
  2.1 0.1 convert_element_type.23
  2.2 0.1 convert_element_type.25
  2.3 0.1 tile.11
  2.4 1.0 %fusion.1.x_ref = bf16[4,2,112,512]{3,2,1,0:T(8,128)(2,1)} fusion(bf16[4,2,1,108]{3,2,1,0:T(2,128)(2,1)S(1)} %tile.11, bf16[4,2,108,512]{3,2,1,0:T(8,128)(2,1)S(1)} %copy.19), kind=kLoop, calls=%fused_computation.2 | loop fusion | flops 2752512 | bytes 1803968 | tf_op jit(solution)/shard_map/concatenate | solution.py:301
  3.4 0.0 copy-done.1
  3.4 0.1 broadcast_in_dim.9
  3.5 0.7 %broadcast_in_dim_reshape.3.qscale_ref = f32[1,512]{1,0:T(1,128)} reshape(f32[8,64]{1,0:T(8,128)S(1)} %broadcast_in_dim.9) | data formatting | bytes 4096 | tf_op jit(solution)/shard_map/broadcast_in_dim;reshape | solution.py:303
  4.1 0.0 copy-done.2
  4.1 0.1 broadcast_in_dim.10
  4.2 0.1 reshape.34
  4.3 0.6 %pad_bitcast_fusion.bias_ref = f32[1,128]{1,0:T(1,128)} fusion(f32[16]{0:T(128)S(1)} %reshape.34), kind=kLoop, calls=%fused_computation.4 | loop fusion | bytes 576 | tf_op jit(solution)/shard_map/broadcast_in_dim | solution.py:304
  4.8 46.2 %window_block.1 = bf16[4,2,112,512]{3,2,1,0:T(8,128)(2,1)} custom-call(bf16[4,2,112,512]{3,2,1,0:T(8,128)(2,1)} %fusion.1.x_ref, f32[1,512]{1,0:T(1,128)} %broadcast_in_dim_reshape.3.qscale_ref, f32[1,128]{1,0:T(1,128)} %pad_bitcast_fusion.bias_ref, bf16[512,1536]{1,0:T(8,128)(2,1)} %wqkv_hbm.1, bf16[512,512]{1,0:T(8,128)(2,1)} %wout_hbm.1, ...), custom_call_target="tpu_custom_call" | custom-call | tf_op jit(solution)/shard_map/window_block/pallas_call | solution.py:308
  51.1 2.1 %copy.20 = bf16[4,2,108,512]{3,1,2,0:T(2,128)(2,1)S(1)} copy(bf16[4,2,108,512]{3,2,1,0:T(8,128)(2,1)} %bitcast.16) | data formatting | bytes 1769472 | tf_op jit(solution)/shard_map/slice | solution.py:338
  53.2 1.6 %copy.21 = bf16[3,2,4,3,2,6,512]{6,1,5,4,3,2,0:T(2,128)(2,1)} copy(bf16[3,2,4,3,2,6,512]{6,4,5,3,1,0,2:T(2,128)(2,1)S(1)} %bitcast.17) | data formatting | bytes 1769472 | tf_op jit(solution)/shard_map/transpose | solution.py:339
  (5 shorter events, 0.0 us)
Async XLA Ops:
  0.0 2.1 %copy-start = (s32[2,12,12]{2,0,1:T(2,128)S(1)}, s32[2,12,12]{2,0,1:T(2,128)}, u32[]{:S(2)}) copy-start(s32[2,12,12]{2,0,1:T(2,128)} %param.9) | copy-start | bytes 3460
  1.9 1.5 %copy-start.1 = (f32[8]{0:T(128)S(1)}, f32[8]{0:T(128)}, u32[]{:S(2)}) copy-start(f32[8]{0:T(128)} %param.12) | copy-start | bytes 100
  1.9 2.2 %copy-start.2 = (f32[8]{0:T(128)S(1)}, f32[8]{0:T(128)}, u32[]{:S(2)}) copy-start(f32[8]{0:T(128)} %param.13) | copy-start | bytes 100

commit v2 on v1

--- a/solution.py
+++ b/solution.py
@@ -36,12 +36,15 @@
 
 def kernel(
     real, heads,
-    x_ref, qscale_ref, bias_ref, wqkv_hbm, wout_hbm, wup_hbm, wdown_hbm,
-    out_ref,
-    wqkv, wout, wup, wdown, win, ret, proj, att, qs, ks, vs, kx,
-    wsem, send1, recv1, send2, recv2,
+    fields_hbm, flags_ref, scale_ref, bias_ref, wqkv_hbm, wout_hbm, wup_hbm, wdown_hbm,
+    out_hbm,
+    raw, x_ref, wqkv, wout, wup, wdown, win, ret, proj, att, qs, ks, vs, kx, acc, out_ref, outs,
+    wsem, osem, send1, recv1, send2, recv2,
 ):
     rows, width = x_ref.shape[2:]
+    groups, levels, _, cells = raw.shape[:4]
+    deep = -(-cells // 16) * 16
+    slabs = groups * levels * SH_LAT
     pair_rows = 2 * rows
     half = 2 * pair_rows
     total = 2 * half
@@ -51,15 +54,6 @@
 
     g, a, b = lax.axis_index("grp"), lax.axis_index("lat"), lax.axis_index("lon")
     na, nb = lax.axis_size("lat"), lax.axis_size("lon")
-
-    weights = [
-        pltpu.make_async_copy(src, dst, wsem.at[i])
-        for i, (src, dst) in enumerate(
-            ((wqkv_hbm, wqkv), (wout_hbm, wout), (wup_hbm, wup), (wdown_hbm, wdown))
-        )
-    ]
-    for copy in weights:
-        copy.start()
 
     barrier = pltpu.get_barrier_semaphore()
     greeted = 0
@@ -78,7 +72,16 @@
                         device_id_type=MESH,
                     )
                     greeted += 1
-    pl.semaphore_wait(barrier, greeted)
+    load = pltpu.make_async_copy(fields_hbm, raw, wsem.at[4])
+    load.start()
+    weights = [
+        pltpu.make_async_copy(src, dst, wsem.at[i])
+        for i, (src, dst) in enumerate(
+            ((wqkv_hbm, wqkv), (wout_hbm, wout), (wup_hbm, wup), (wdown_hbm, wdown))
+        )
+    ]
+    for copy in weights:
+        copy.start()
 
     def parity_to(d, cc):
         return (g + d + b + cc) % 2
@@ -86,14 +89,14 @@
     def row_of(parity, rr):
         return (1 + 2 * parity + rr) % 4
 
-    def forward(d, cc, rr, act):
-        parity = parity_to(d, cc)
-        r = row_of(parity, rr)
+    def forward(r, c, act):
+        parity, rr = (1, 1) if r == 0 else ((r - 1) // 2, (r - 1) % 2)
+        cc = 1 - c
+        d = (parity + g + b + cc) % 2
         p = 2 * d + cc
-        src = x_ref.at[r, 1 - cc]
+        src = x_ref.at[r, c]
         dst = win.at[p, rr]
         i = 2 * p + rr
-        edge = rr * parity
 
         def local():
             return pltpu.make_async_copy(src, dst, recv1.at[i])
@@ -103,13 +106,24 @@
                 src_ref=src, dst_ref=dst, send_sem=send1.at[i], recv_sem=recv1.at[i],
                 device_id={
                     "grp": (g + d) % 2,
-                    "lat": (a - edge + na) % na,
+                    "lat": (a - 1 + na) % na if r == 0 else a,
                     "lon": (b - cc + nb) % nb,
                 },
                 device_id_type=MESH,
             )
 
-        act(d, cc, rr, parity, local, remote)
+        if r == 0 or cc:
+            act(remote())
+        else:
+            pl.when(d == 1)(lambda: act(remote()))
+            if act is begin:
+                pl.when(d == 0)(lambda: act(local()))
+
+    def begin(copy):
+        copy.start()
+
+    def drain(copy):
+        copy.wait_send()
 
     def backward(d, cc, rr, act):
         parity = (g + b) % 2
@@ -150,16 +164,52 @@
         elif rr == 1:
             pl.when(parity == 1)(lambda: remote().wait_send())
 
-    for d, cc in ((1, 0), (1, 1), (0, 1), (0, 0)):
-        for rr in (1, 0):
-            forward(d, cc, rr, start)
+    token = iota((2 * rows, 1), 0)
+    inside = token % rows
+    place = jnp.where(
+        inside < real, inside // SH_LON * deep + inside % SH_LON + token // rows * SH_LON, -1
+    )
+    pick = jnp.where(iota((2 * rows, slabs * deep), 1) == place, 1.0, 0.0).astype(BF16)
+
+    load.wait()
+    order = (0, 3, 1, 2)
+    empty = jnp.zeros((deep - cells, width), BF16)
+
+    def sort_row(r):
+        pieces = []
+        for gl in range(groups * levels):
+            for i in range(SH_LAT):
+                pieces += [raw[gl // levels, gl % levels, SH_LAT * r + i], empty]
+        sorted_rows = dot(pick, jnp.concatenate(pieces, 0)).astype(BF16)
+        for c in (0, 1):
+            x_ref[r, c] = sorted_rows[c * rows : (c + 1) * rows]
+            x_ref[r, c, rows - 16 :, :128] = (
+                sorted_rows[(c + 1) * rows - 16 : (c + 1) * rows, :128] + flags_ref[r, c]
+            )
+
+    sort_row(order[0])
+    with jax.named_scope("greet"):
+        pl.semaphore_wait(barrier, greeted)
+    for k in range(4):
+        if k < 3:
+            sort_row(order[k + 1])
+        for c in (0, 1):
+            forward(order[k], c, begin)
 
     last = jnp.where(a == na - 1, (g + b) % 2, 0)
     row_in_block = iota((pair_rows, lanes), 0) % rows
     valid = row_in_block < real
     lane = iota((pair_rows, lanes), 1)
     late = jnp.where(iota((pair_rows, lanes), 0) >= rows, last, 0)
-    raw_bias = bias_ref[...]
+    raw_bias = jnp.zeros((1, lanes), F32)
+    qscale = jnp.zeros((1, width), F32)
+    for h in range(heads):
+        raw_bias = jnp.where(
+            iota((1, lanes), 1) // 2 == h, bias_ref[h] * LOG2E, raw_bias
+        )
+        qscale = jnp.where(
+            iota((1, width), 1) // head_size == h, scale_ref[h] * (LOG2E / head_size), qscale
+        )
     bias_hi = raw_bias.astype(BF16).astype(F32)
     bias_row = jnp.where(iota(raw_bias.shape, 1) % 2 == 0, bias_hi, raw_bias - bias_hi)
     far = jnp.where(
@@ -174,11 +224,13 @@
     eye = jnp.where(iota((rows, lanes), 0) == iota((rows, lanes), 1), 1.0, 0.0).astype(BF16)
     ones = jnp.where(valid, 1.0, 0.0).astype(BF16)
 
-    weights[0].wait()
+    with jax.named_scope("wait_w"):
+        weights[0].wait()
 
     def project(p, carry):
-        for rr in (0, 1):
-            pltpu.make_async_copy(win.at[p, rr], win.at[p, rr], recv1.at[2 * p + rr]).wait()
+        with jax.named_scope("wait_in"):
+            for rr in (0, 1):
+                pltpu.make_async_copy(win.at[p, rr], win.at[p, rr], recv1.at[2 * p + rr]).wait()
         both = win[p].reshape(pair_rows, width)
         normed = layer_norm(both.astype(F32)).astype(BF16)
         here = pl.ds(p * pair_rows, pair_rows)
@@ -189,7 +241,7 @@
                 square = dot((mixed * mixed).astype(BF16), blocks)
                 unit = mixed * lax.rsqrt(square + 1e-06)
                 if part == 0:
-                    unit = unit * qscale_ref[:, lo : lo + span]
+                    unit = unit * qscale[:, lo : lo + span]
                 unit = unit.astype(BF16)
                 store[2 * s, here] = unit[:, :lanes]
                 store[2 * s + 1, here] = unit[:, lanes:]
@@ -210,49 +262,81 @@
         kx[here] = (marks * bias_row + far).astype(BF16)
         return carry
 
-    lax.fori_loop(0, 4, project, 0)
-    weights[1].wait()
-
-    q_lane = iota((half, lanes), 1)
-    q_late = jnp.where((iota((half, lanes), 0) // rows) % 2 == 1, last, 0)
-    q_region = jnp.where(
-        q_lane == 2 * heads, (1 - q_late).astype(F32),
-        jnp.where(q_lane == 2 * heads + 1, q_late.astype(F32), 0.0),
-    )
-    low = q_lane < head_size
-    ones_all = jnp.concatenate([ones] * (total // pair_rows), 0)
-
-    for d in (1, 0):
-
-        def attend(pair, carry):
-            query = qs[pair, d * half : (d + 1) * half]
-            keys = jnp.concatenate([ks[pair], kx[...]], 1)
-            values = jnp.concatenate([vs[pair], ones_all], 1)
+    def attend(q0, nq, k0, nk, first, final):
+        q_lane = iota((nq, lanes), 1)
+        q_late = jnp.where((iota((nq, lanes), 0) // rows) % 2 == 1, last, 0)
+        q_region = jnp.where(
+            q_lane == 2 * heads, (1 - q_late).astype(F32),
+            jnp.where(q_lane == 2 * heads + 1, q_late.astype(F32), 0.0),
+        )
+        low = q_lane < head_size
+        sides = [
+            jnp.where(low if e == 0 else ~low, 1.0, 0.0).astype(BF16) for e in (0, 1)
+        ]
+        ones_all = jnp.concatenate([ones] * (nk // pair_rows), 0)
+
+        def one_pair(pair, carry):
+            query = qs[pair, q0 : q0 + nq]
+            keys = jnp.concatenate([ks[pair, k0 : k0 + nk], kx[k0 : k0 + nk]], 1)
+            values = jnp.concatenate([vs[pair, k0 : k0 + nk], ones_all], 1)
+            asked = [
+                jnp.concatenate(
+                    [
+                        query * sides[e],
+                        jnp.where(q_lane // 2 == 2 * pair + e, 1.0, q_region).astype(BF16),
+                    ],
+                    1,
+                )
+                for e in (0, 1)
+            ]
+            if nq == pair_rows:
+                summed = dot(jnp.exp2(dot_t(jnp.concatenate(asked, 0), keys)).astype(BF16), values)
+                parts = [summed[:nq], summed[nq:]]
+            else:
+                parts = [dot(jnp.exp2(dot_t(ask, keys)).astype(BF16), values) for ask in asked]
             ratios = []
             for e in (0, 1):
-                chosen = jnp.where(low if e == 0 else ~low, query.astype(F32), 0.0).astype(BF16)
-                extra = jnp.where(q_lane // 2 == 2 * pair + e, 1.0, q_region).astype(BF16)
-                scores = dot_t(jnp.concatenate([chosen, extra], 1), keys)
-                summed = dot(jnp.exp2(scores).astype(BF16), values)
-                ratios.append(summed[:, :lanes] / summed[:, lanes:])
-            att[:, pl.ds(pl.multiple_of(pair * lanes, lanes), lanes)] = jnp.where(
-                low, ratios[0], ratios[1]
-            ).astype(BF16)
+                if not first:
+                    parts[e] = parts[e] + acc[pair, e]
+                if not final:
+                    acc[pair, e] = parts[e]
+                else:
+                    ratios.append(parts[e][:, :lanes] / parts[e][:, lanes:])
+            if final:
+                att[:nq, pl.ds(pl.multiple_of(pair * lanes, lanes), lanes)] = jnp.where(
+                    low, ratios[0], ratios[1]
+                ).astype(BF16)
             return carry
 
-        lax.fori_loop(0, pairs, attend, 0)
-        projected = dot(att[...], wout[...]).astype(BF16)
-        proj[2 * d : 2 * d + 2] = projected.reshape(2, 2, rows, width)
-        for cc in (1, 0):
-            for rr in (1, 0):
-                backward(d, cc, rr, start)
+        with jax.named_scope("attend"):
+            lax.fori_loop(0, pairs, one_pair, 0)
+
+    lax.fori_loop(0, 2, project, 0)
+    attend(0, half, 0, half, True, False)
+    lax.fori_loop(2, 4, project, 0)
+    weights[1].wait()
+
+    for p in (3, 2):
+        attend(p * pair_rows, pair_rows, 0, total, True, True)
+        projected = dot(att[:pair_rows], wout[...]).astype(BF16)
+        proj[p] = projected.reshape(2, rows, width)
+        for rr in (1, 0):
+            backward(1, p % 2, rr, start)
+    attend(0, half, half, half, False, True)
+    projected = dot(att[...], wout[...]).astype(BF16)
+    proj[:2] = projected.reshape(2, 2, rows, width)
+    for cc in (1, 0):
+        for rr in (1, 0):
+            backward(0, cc, rr, start)
 
     weights[2].wait()
     weights[3].wait()
 
-    def join(p, carry):
-        for rr in (0, 1):
-            pltpu.make_async_copy(ret.at[p, rr], ret.at[p, rr], recv2.at[2 * p + rr]).wait()
+    def join(step, carry):
+        p = jnp.where(step < 2, step, 5 - step)
+        with jax.named_scope("wait_back"):
+            for rr in (0, 1):
+                pltpu.make_async_copy(ret.at[p, rr], ret.at[p, rr], recv2.at[2 * p + rr]).wait()
         d, cc = p // 2, p % 2
         parity = parity_to(d, cc)
         r0, r1 = row_of(parity, 0), row_of(parity, 1)
@@ -271,15 +355,43 @@
         joined = joined.astype(BF16)
         out_ref[r0, 1 - cc] = joined[:rows]
         out_ref[r1, 1 - cc] = joined[rows:]
+
+        @pl.when(d == 1)
+        def _():
+            for k, r in enumerate((r0, r1)):
+                ordered = dot(put, out_ref[r].reshape(2 * rows, width)).astype(BF16)
+                for gl in range(groups * levels):
+                    for i in range(SH_LAT):
+                        lo = (gl * SH_LAT + i) * deep
+                        outs[gl // levels, gl % levels, SH_LAT * r + i] = ordered[lo : lo + cells]
+                deliver(r, 2 * cc + k).start()
+
         return carry
 
+    def deliver(r, i):
+        part = pl.ds(SH_LAT * r, SH_LAT)
+        return pltpu.make_async_copy(outs.at[:, :, part], out_hbm.at[:, :, part], osem.at[i])
+
+    token = iota((1, 2 * rows), 1)
+    inside = token % rows
+    place = jnp.where(
+        inside < real, inside // SH_LON * deep + inside % SH_LON + token // rows * SH_LON, -1
+    )
+    put = jnp.where(iota((slabs * deep, 2 * rows), 0) == place, 1.0, 0.0).astype(BF16)
+
     lax.fori_loop(0, 4, join, 0)
 
-    for d in (0, 1):
+    with jax.named_scope("drain"):
+        for c in (0, 1):
+            for r in range(4):
+                forward(r, c, drain)
+        for d in (0, 1):
+            for cc in (0, 1):
+                for rr in (0, 1):
+                    backward(d, cc, rr, finish)
         for cc in (0, 1):
-            for rr in (0, 1):
-                forward(d, cc, rr, finish)
-                backward(d, cc, rr, finish)
+            for k in (0, 1):
+                deliver(row_of(parity_to(1, cc), k), 2 * cc + k).wait()
 
 
 def per_device(fields, surface_mask, w_qkv, w_out, logit_scale, mask_bias, w_up, w_down):
@@ -292,25 +404,24 @@
     rows = -(-(real + 1) // 16) * 16
     total = 8 * rows
 
-    split = fields.reshape(groups, levels, tris, SH_LAT, sides, SH_LON, width)
-    tokens = jnp.transpose(split, (2, 4, 0, 1, 3, 5, 6)).reshape(tris, sides, real, width)
     flags = surface_mask.reshape(levels, tris, SH_LAT, sides, SH_LON)
     flags = jnp.transpose(flags, (1, 3, 0, 2, 4)).reshape(tris, sides, 1, real // groups)
     flags = jnp.tile(flags.astype(BF16), (1, 1, 1, groups))
-    flags = jnp.pad(flags, ((0, 0), (0, 0), (0, rows - real - 1), (0, width - real)))
-    x = jnp.concatenate([tokens, flags], 2)
-
-    qscale = jnp.repeat(logit_scale * (LOG2E / head_size), head_size)[None]
-    bias = jnp.pad(jnp.repeat(mask_bias * LOG2E, 2), (0, 2 * head_size - 2 * heads))[None]
+    flags = jnp.pad(
+        flags, ((0, 0), (0, 0), (real - rows + 16, rows - real - 1), (0, 128 - real))
+    )
 
     vmem = pl.BlockSpec(memory_space=pltpu.VMEM)
+    scalars = pl.BlockSpec(memory_space=pltpu.SMEM)
     anywhere = pl.BlockSpec(memory_space=pl.ANY)
-    joined = pl.pallas_call(
+    return pl.pallas_call(
         functools.partial(kernel, real, heads),
-        out_shape=jax.ShapeDtypeStruct(x.shape, BF16),
-        in_specs=[vmem] * 3 + [anywhere] * 4,
-        out_specs=vmem,
+        out_shape=jax.ShapeDtypeStruct(fields.shape, BF16),
+        in_specs=[anywhere, vmem, scalars, scalars] + [anywhere] * 4,
+        out_specs=anywhere,
         scratch_shapes=[
+            pltpu.VMEM(fields.shape, BF16),
+            pltpu.VMEM((tris, sides, rows, width), BF16),
             pltpu.VMEM(w_qkv.shape, BF16),
             pltpu.VMEM(w_out.shape, BF16),
             pltpu.VMEM(w_up.shape, BF16),
@@ -323,6 +434,10 @@
             pltpu.VMEM((heads // 2, total, 2 * head_size), BF16),
             pltpu.VMEM((heads // 2, total, 2 * head_size), BF16),
             pltpu.VMEM((total, 2 * head_size), BF16),
+            pltpu.VMEM((heads // 2, 2, total // 2, 4 * head_size), F32),
+            pltpu.VMEM((tris, sides, rows, width), BF16),
+            pltpu.VMEM(fields.shape, BF16),
+            pltpu.SemaphoreType.DMA((5,)),
             pltpu.SemaphoreType.DMA((4,)),
             pltpu.SemaphoreType.DMA((8,)),
             pltpu.SemaphoreType.DMA((8,)),
@@ -333,10 +448,7 @@
             collective_id=0, has_side_effects=True, vmem_limit_bytes=56 * 1024 * 1024
         ),
         name="window_block",
-    )(x, qscale, bias, w_qkv, w_out, w_up, w_down)
-
-    kept = joined[:, :, :real].reshape(tris, sides, groups, levels, SH_LAT, SH_LON, width)
-    return jnp.transpose(kept, (2, 3, 0, 4, 1, 5, 6)).reshape(fields.shape)
+    )(fields, flags, logit_scale, mask_bias, w_qkv, w_out, w_up, w_down)
 
 
 def solution(mesh):

time: 55 us -> 55.8 us (1.015)
  Pallas kernels: 46.2 us -> 48.4 us
  local copies, waits for them, and re-layouts: 7.49 us -> 6.42 us
    pallas_call x0 -> x1, local copies, waits for them, and re-layouts: none -> 3.09 us  [per_device(): pl.pallas_call(functools.partial(kernel, real, heads), out_shape=jax.Shap...]
    unnamed x6 -> x1, local copies, waits for them, and re-layouts: 0.02 us -> 2.41 us
    pallas_call x1, Pallas kernels: 46.2 us -> 48.4 us  [per_device(): pl.pallas_call(functools.partial(kernel, real, heads), out_shape=jax.Shap...]
    reshape x3 -> x0, local copies, waits for them, and re-layouts: 2.09 us -> none  [the longest x1 1.86 us: per_device(): split = fields.reshape(groups, levels, tris, SH_LAT, sides, SH_LON, width)]
    slice x1 -> x0, local copies, waits for them, and re-layouts: 2.09 us -> none  [per_device(): joined[:, :, :real]]
    transpose x1 -> x0, local copies, waits for them, and re-layouts: 1.64 us -> none  [per_device(): return jnp.transpose(kept, (2, 3, 0, 4, 1, 5, 6)).reshape(fields.shape)]
    concatenate x1 -> x0, other arithmetic: 1.02 us -> none  [per_device(): x = jnp.concatenate([tokens, flags], 2)]
    broadcast_in_dim x3 -> x0, local copies, waits for them, and re-layouts: 0.72 us -> none  [the longest x1 0.57 us: per_device(): jnp.pad(jnp.repeat(mask_bias * LOG2E, 2), (0, 2 * head_size - 2 * heads))]
where the time goes in v2:
time: 55.8 us; the launch traced here: 55.5 us
  Pallas kernels  48.4 us (87%)
  local copies, waits for them, and re-layouts  6.42 us (12%)
  other arithmetic  0.71 us (1%)
    pallas_call x1, Pallas kernels, per_device(): pl.pallas_call(functools.partial(kernel, real, heads), out_shape=jax.Shap...  48.4 us
    pallas_call x1, local copies, waits for them, and re-layouts, per_device(): pl.pallas_call(functools.partial(kernel, real, heads), out_shape=jax.Shap...  3.09 us
    unnamed x1, local copies, waits for them, and re-layouts  2.41 us

profile of v2, /device:TPU:1, one launch (start us, length us, event | category | flops | bytes accessed | tf_op | source)
XLA Modules:
  0.0 55.5 jit_solution(1276763467033604464)
XLA Ops:
  0.0 0.7 %convert_element_type.20 = bf16[2,12,12]{2,0,1:T(2,128)(2,1)S(1)} convert(s32[2,12,12]{2,0,1:T(2,128)} %param.9) | non-fusion elementwise | flops 288 | bytes 1728 | tf_op jit(solution)/shard_map/convert_element_type | solution.py:409
  0.7 0.1 convert_element_type.21
  0.8 0.1 convert_element_type.23
  0.9 0.1 tile.11
  1.0 0.6 %pad.4.flags_ref = bf16[4,2,16,128]{3,2,1,0:T(8,128)(2,1)} pad(bf16[4,2,1,108]{3,2,1,0:T(2,128)(2,1)S(1)} %tile.11, bf16[]{:T(256)} %constant.2.clone.1), padding=0_0x0_0x12_3x0_20 | pad | bytes 34498 | tf_op jit(solution)/shard_map/jit(_pad)/pad | solution.py:410
  1.6 2.4 %copy.13.fields_hbm = bf16[3,2,12,12,512]{4,3,2,1,0:T(8,128)(2,1)} copy(bf16[3,2,12,12,512]{4,1,3,2,0:T(2,128)(2,1)} %param.8) | data formatting | bytes 1769472 | tf_op args[0]
  4.0 48.4 %window_block.1 = bf16[3,2,12,12,512]{4,3,2,1,0:T(8,128)(2,1)} custom-call(bf16[3,2,12,12,512]{4,3,2,1,0:T(8,128)(2,1)} %copy.13.fields_hbm, bf16[4,2,16,128]{3,2,1,0:T(8,128)(2,1)} %pad.4.flags_ref, f32[8]{0:T(128)} %scale_ref.1, f32[8]{0:T(128)} %bias_ref.1, bf16[512,1536]{1,0:T(8,128)(2,1)} %wqkv_hbm.1, bf16[512,512]{1,0:T(8,128)(2,1)} %wout_hbm.1, ...), custom_call_target="tpu_custom_call" | custom-call | tf_op jit(solution)/shard_map/window_block/pallas_call | solution.py:417
  52.4 3.1 %copy.14 = bf16[3,2,12,12,512]{4,1,3,2,0:T(2,128)(2,1)} copy(bf16[3,2,12,12,512]{4,3,2,1,0:T(8,128)(2,1)} %window_block.1) | data formatting | bytes 1769472 | tf_op jit(solution)/shard_map/window_block/pallas_call | solution.py:417
  (2 shorter events, 0.0 us)

commit v3 on v2

--- a/solution.py
+++ b/solution.py
@@ -36,15 +36,17 @@
 
 def kernel(
     real, heads,
-    fields_hbm, flags_ref, scale_ref, bias_ref, wqkv_hbm, wout_hbm, wup_hbm, wdown_hbm,
+    fields_hbm, mask_ref, scale_ref, bias_ref, wqkv_hbm, wout_hbm, wup_hbm, wdown_hbm,
     out_hbm,
-    raw, x_ref, wqkv, wout, wup, wdown, win, ret, proj, att, qs, ks, vs, kx, acc, out_ref, outs,
+    raw, tidy, x_ref, wqkv, wout, wup, wdown, win, ret, proj, att, qs, ks, vs, kx, acc, outs,
     wsem, osem, send1, recv1, send2, recv2,
 ):
     rows, width = x_ref.shape[2:]
-    groups, levels, _, cells = raw.shape[:4]
-    deep = -(-cells // 16) * 16
-    slabs = groups * levels * SH_LAT
+    groups, nlat, lon_pairs, sub = raw.shape[:4]
+    levels = mask_ref.shape[1]
+    tiles = width // 128
+    side_pairs = SH_LON // 2
+    slab_rows = groups * SH_LAT * side_pairs * sub
     pair_rows = 2 * rows
     half = 2 * pair_rows
     total = 2 * half
@@ -164,28 +166,47 @@
         elif rr == 1:
             pl.when(parity == 1)(lambda: remote().wait_send())
 
-    token = iota((2 * rows, 1), 0)
-    inside = token % rows
+    span_of = iota((tiles * rows, 1), 0)
+    inside = span_of % rows
     place = jnp.where(
-        inside < real, inside // SH_LON * deep + inside % SH_LON + token // rows * SH_LON, -1
+        inside < real,
+        inside // levels * (tiles * levels) + span_of // rows * levels + inside % levels,
+        -1,
     )
-    pick = jnp.where(iota((2 * rows, slabs * deep), 1) == place, 1.0, 0.0).astype(BF16)
-
-    load.wait()
+    pick = jnp.where(iota((tiles * rows, slab_rows), 1) == place, 1.0, 0.0).astype(BF16)
+
+    tidy[...] = jnp.zeros_like(tidy)
+    for i in range(nlat):
+        tidy[levels * i : levels * (i + 1), : mask_ref.shape[2]] = mask_ref[i].astype(F32)
+    spot = iota((8 * 128, 1), 0)
+    block, inside = spot // 128, spot % 128
+    cell = inside // levels
+    at_lat = block // 2 * SH_LAT + cell // SH_LON % SH_LAT
+    at_lat = at_lat * levels + inside % levels
+    at_lon = block % 2 * SH_LON + cell % SH_LON
+    at_lat = jnp.where(inside < real, at_lat, -1)
+    by_lat = jnp.where(iota((8 * 128, tidy.shape[0]), 1) == at_lat, 1.0, 0.0).astype(BF16)
+    by_cell = dot(by_lat, tidy[...].astype(BF16))
+    by_cell = jnp.where(iota((8 * 128, 128), 1) == at_lon, by_cell, 0.0).astype(BF16)
+    flags = dot_t(jnp.ones((16, 128), BF16), by_cell)
+    flag_row = iota((16, 128), 0) == real - rows + 16
+
+    with jax.named_scope("load"):
+        load.wait()
     order = (0, 3, 1, 2)
-    empty = jnp.zeros((deep - cells, width), BF16)
 
     def sort_row(r):
-        pieces = []
-        for gl in range(groups * levels):
-            for i in range(SH_LAT):
-                pieces += [raw[gl // levels, gl % levels, SH_LAT * r + i], empty]
-        sorted_rows = dot(pick, jnp.concatenate(pieces, 0)).astype(BF16)
         for c in (0, 1):
-            x_ref[r, c] = sorted_rows[c * rows : (c + 1) * rows]
-            x_ref[r, c, rows - 16 :, :128] = (
-                sorted_rows[(c + 1) * rows - 16 : (c + 1) * rows, :128] + flags_ref[r, c]
-            )
+            piece = raw[:, SH_LAT * r : SH_LAT * (r + 1), side_pairs * c : side_pairs * (c + 1)]
+            tall = dot(pick, piece.reshape(slab_rows, 128)).astype(BF16)
+            for t in range(tiles):
+                x_ref[r, c, :, 128 * t : 128 * (t + 1)] = tall[t * rows : (t + 1) * rows]
+            k = 2 * r + c
+            x_ref[r, c, rows - 16 :, :128] = jnp.where(
+                flag_row,
+                flags[:, 128 * k : 128 * (k + 1)],
+                tall[rows - 16 : rows].astype(F32),
+            ).astype(BF16)
 
     sort_row(order[0])
     with jax.named_scope("greet"):
@@ -344,40 +365,40 @@
         back = ret[p].reshape(pair_rows, width)
         residual = (own.astype(F32) + back.astype(F32)).astype(BF16).astype(F32)
         mlp_in = layer_norm(residual).astype(BF16)
-        joined = residual
+        update = jnp.zeros_like(residual)
         hidden_size = wup.shape[1]
         piece = 512
         for s in range(hidden_size // piece):
             up = dot(mlp_in, wup[:, s * piece : (s + 1) * piece])
-            inner = math.sqrt(2.0 / math.pi) * (up + 0.044715 * (up * up * up))
-            hidden = (0.5 * up * (1.0 + jnp.tanh(inner))).astype(BF16)
-            joined = joined + dot(hidden, wdown[s * piece : (s + 1) * piece, :])
-        joined = joined.astype(BF16)
-        out_ref[r0, 1 - cc] = joined[:rows]
-        out_ref[r1, 1 - cc] = joined[rows:]
-
-        @pl.when(d == 1)
-        def _():
-            for k, r in enumerate((r0, r1)):
-                ordered = dot(put, out_ref[r].reshape(2 * rows, width)).astype(BF16)
-                for gl in range(groups * levels):
-                    for i in range(SH_LAT):
-                        lo = (gl * SH_LAT + i) * deep
-                        outs[gl // levels, gl % levels, SH_LAT * r + i] = ordered[lo : lo + cells]
-                deliver(r, 2 * cc + k).start()
-
+            slope = math.sqrt(2.0 / math.pi)
+            bent = jnp.tanh(up * (slope + 0.044715 * slope * (up * up)))
+            twice = (up + up * bent).astype(BF16)
+            update = update + dot(twice, wdown[s * piece : (s + 1) * piece, :])
+        joined = (residual + 0.5 * update).astype(BF16)
+        for k, r in enumerate((r0, r1)):
+            own_rows = joined[k * rows : (k + 1) * rows]
+            tall = jnp.concatenate(
+                [own_rows[:, 128 * t : 128 * (t + 1)] for t in range(tiles)], 0
+            )
+            i = 2 * p + k
+            outs[i] = dot(put, tall).astype(BF16).reshape(outs.shape[1:])
+            deliver(r, 1 - cc, i).start()
         return carry
 
-    def deliver(r, i):
-        part = pl.ds(SH_LAT * r, SH_LAT)
-        return pltpu.make_async_copy(outs.at[:, :, part], out_hbm.at[:, :, part], osem.at[i])
-
-    token = iota((1, 2 * rows), 1)
-    inside = token % rows
+    def deliver(r, c, i):
+        rim = pl.ds(SH_LAT * r, SH_LAT)
+        return pltpu.make_async_copy(
+            outs.at[i], out_hbm.at[:, rim, pl.ds(side_pairs * c, side_pairs)], osem.at[i]
+        )
+
+    span_of = iota((1, tiles * rows), 1)
+    inside = span_of % rows
     place = jnp.where(
-        inside < real, inside // SH_LON * deep + inside % SH_LON + token // rows * SH_LON, -1
+        inside < real,
+        inside // levels * (tiles * levels) + span_of // rows * levels + inside % levels,
+        -1,
     )
-    put = jnp.where(iota((slabs * deep, 2 * rows), 0) == place, 1.0, 0.0).astype(BF16)
+    put = jnp.where(iota((slab_rows, tiles * rows), 0) == place, 1.0, 0.0).astype(BF16)
 
     lax.fori_loop(0, 4, join, 0)
 
@@ -389,9 +410,10 @@
             for cc in (0, 1):
                 for rr in (0, 1):
                     backward(d, cc, rr, finish)
-        for cc in (0, 1):
+        for p in range(4):
             for k in (0, 1):
-                deliver(row_of(parity_to(1, cc), k), 2 * cc + k).wait()
+                r = row_of(parity_to(p // 2, p % 2), k)
+                deliver(r, 1 - p % 2, 2 * p + k).wait()
 
 
 def per_device(fields, surface_mask, w_qkv, w_out, logit_scale, mask_bias, w_up, w_down):
@@ -404,23 +426,22 @@
     rows = -(-(real + 1) // 16) * 16
     total = 8 * rows
 
-    flags = surface_mask.reshape(levels, tris, SH_LAT, sides, SH_LON)
-    flags = jnp.transpose(flags, (1, 3, 0, 2, 4)).reshape(tris, sides, 1, real // groups)
-    flags = jnp.tile(flags.astype(BF16), (1, 1, 1, groups))
-    flags = jnp.pad(
-        flags, ((0, 0), (0, 0), (real - rows + 16, rows - real - 1), (0, 128 - real))
-    )
+    tiles = width // 128
+    raw = fields.reshape(groups, levels, nlat, nlon, tiles, 128)
+    raw = jnp.transpose(raw, (0, 2, 3, 4, 1, 5))
+    raw = raw.reshape(groups, nlat, nlon // 2, 2 * tiles * levels, 128)
 
     vmem = pl.BlockSpec(memory_space=pltpu.VMEM)
     scalars = pl.BlockSpec(memory_space=pltpu.SMEM)
     anywhere = pl.BlockSpec(memory_space=pl.ANY)
-    return pl.pallas_call(
+    joined = pl.pallas_call(
         functools.partial(kernel, real, heads),
-        out_shape=jax.ShapeDtypeStruct(fields.shape, BF16),
+        out_shape=jax.ShapeDtypeStruct(raw.shape, BF16),
         in_specs=[anywhere, vmem, scalars, scalars] + [anywhere] * 4,
         out_specs=anywhere,
         scratch_shapes=[
-            pltpu.VMEM(fields.shape, BF16),
+            pltpu.VMEM(raw.shape, BF16),
+            pltpu.VMEM((nlat * levels, 128), F32),
             pltpu.VMEM((tris, sides, rows, width), BF16),
             pltpu.VMEM(w_qkv.shape, BF16),
             pltpu.VMEM(w_out.shape, BF16),
@@ -435,10 +456,9 @@
             pltpu.VMEM((heads // 2, total, 2 * head_size), BF16),
             pltpu.VMEM((total, 2 * head_size), BF16),
             pltpu.VMEM((heads // 2, 2, total // 2, 4 * head_size), F32),
-            pltpu.VMEM((tris, sides, rows, width), BF16),
-            pltpu.VMEM(fields.shape, BF16),
+            pltpu.VMEM((8, groups, SH_LAT, SH_LON // 2) + raw.shape[3:], BF16),
             pltpu.SemaphoreType.DMA((5,)),
-            pltpu.SemaphoreType.DMA((4,)),
+            pltpu.SemaphoreType.DMA((8,)),
             pltpu.SemaphoreType.DMA((8,)),
             pltpu.SemaphoreType.DMA((8,)),
             pltpu.SemaphoreType.DMA((8,)),
@@ -448,7 +468,10 @@
             collective_id=0, has_side_effects=True, vmem_limit_bytes=56 * 1024 * 1024
         ),
         name="window_block",
-    )(fields, flags, logit_scale, mask_bias, w_qkv, w_out, w_up, w_down)
+    )(raw, jnp.transpose(surface_mask, (1, 0, 2)), logit_scale, mask_bias, w_qkv, w_out, w_up, w_down)
+
+    joined = joined.reshape(groups, nlat, nlon, tiles, levels, 128)
+    return jnp.transpose(joined, (0, 4, 1, 2, 3, 5)).reshape(fields.shape)
 
 
 def solution(mesh):

time: 55.8 us -> 51.6 us (0.925)
  local copies, waits for them, and re-layouts: 6.42 us -> 2.76 us
  other arithmetic: 0.71 us -> 0 us
    pallas_call x1 -> x0, local copies, waits for them, and re-layouts: 3.09 us -> none  [per_device(): pl.pallas_call(functools.partial(kernel, real, heads), out_shape=jax.Shap...]
    convert_element_type x1 -> x0, other arithmetic: 0.71 us -> none  [per_device(): flags = jnp.tile(flags.astype(BF16), (1, 1, 1, groups))]
    pad x1 -> x0, local copies, waits for them, and re-layouts: 0.63 us -> none  [per_device(): jnp.pad(flags, ((0, 0), (0, 0), (real - rows + 16, rows - real - 1), (0,...]
where the time goes in v3:
time: 51.6 us; the launch traced here: 51.3 us
  Pallas kernels  48.6 us (94%)
  local copies, waits for them, and re-layouts  2.76 us (5%)
    pallas_call x1, Pallas kernels, per_device(): pl.pallas_call(functools.partial(kernel, real, heads), out_shape=jax.Shap...  48.6 us
    unnamed x1, local copies, waits for them, and re-layouts  2.76 us

profile of v3, /device:TPU:1, one launch (start us, length us, event | category | flops | bytes accessed | tf_op | source)
XLA Modules:
  0.0 51.3 jit_solution(3099079930920549357)
XLA Ops:
  0.0 48.6 %window_block.1 = bf16[3,12,6,16,128]{4,3,2,1,0:T(8,128)(2,1)} custom-call(bf16[3,12,6,16,128]{4,3,2,1,0:T(8,128)(2,1)} %bitcast.12, s32[12,2,12]{2,1,0:T(2,128)} %bitcast.13, f32[8]{0:T(128)} %scale_ref.1, f32[8]{0:T(128)} %bias_ref.1, bf16[512,1536]{1,0:T(8,128)(2,1)} %wqkv_hbm.1, bf16[512,512]{1,0:T(8,128)(2,1)} %wout_hbm.1, bf16[512,2048]{1,0:T(8,128)(2,1)} %wup_hbm.1, ...), custom_call_target="tpu_custom_call" | custom-call | tf_op jit(solution)/shard_map/window_block/pallas_call | solution.py:437
  48.6 2.8 %copy.12 = bf16[3,2,12,12,512]{4,1,3,2,0:T(2,128)(2,1)} copy(bf16[3,2,12,12,512]{4,1,3,2,0:T(2,128)(2,1)} %bitcast.11) | data formatting | bytes 1769472

commit v4 on v3

--- a/solution.py
+++ b/solution.py
@@ -91,12 +91,11 @@
     def row_of(parity, rr):
         return (1 + 2 * parity + rr) % 4
 
-    def forward(r, c, act):
+    def forward(r, d, act):
         parity, rr = (1, 1) if r == 0 else ((r - 1) // 2, (r - 1) % 2)
-        cc = 1 - c
-        d = (parity + g + b + cc) % 2
+        cc = (parity + g + b + d) % 2
         p = 2 * d + cc
-        src = x_ref.at[r, c]
+        src = x_ref.at[r, 1 - cc]
         dst = win.at[p, rr]
         i = 2 * p + rr
 
@@ -114,12 +113,12 @@
                 device_id_type=MESH,
             )
 
-        if r == 0 or cc:
+        if r == 0 or d:
             act(remote())
         else:
-            pl.when(d == 1)(lambda: act(remote()))
+            pl.when(cc == 1)(lambda: act(remote()))
             if act is begin:
-                pl.when(d == 0)(lambda: act(local()))
+                pl.when(cc == 0)(lambda: act(local()))
 
     def begin(copy):
         copy.start()
@@ -214,8 +213,10 @@
     for k in range(4):
         if k < 3:
             sort_row(order[k + 1])
-        for c in (0, 1):
-            forward(order[k], c, begin)
+        forward(order[k], 0, begin)
+        if k:
+            forward(order[k - 1], 1, begin)
+    forward(order[3], 1, begin)
 
     last = jnp.where(a == na - 1, (g + b) % 2, 0)
     row_in_block = iota((pair_rows, lanes), 0) % rows
@@ -337,18 +338,21 @@
     lax.fori_loop(2, 4, project, 0)
     weights[1].wait()
 
-    for p in (3, 2):
+    def far_queries(p):
         attend(p * pair_rows, pair_rows, 0, total, True, True)
         projected = dot(att[:pair_rows], wout[...]).astype(BF16)
         proj[p] = projected.reshape(2, rows, width)
         for rr in (1, 0):
             backward(1, p % 2, rr, start)
+
+    far_queries(3)
     attend(0, half, half, half, False, True)
     projected = dot(att[...], wout[...]).astype(BF16)
     proj[:2] = projected.reshape(2, 2, rows, width)
     for cc in (1, 0):
         for rr in (1, 0):
             backward(0, cc, rr, start)
+    far_queries(2)
 
     weights[2].wait()
     weights[3].wait()
@@ -403,9 +407,9 @@
     lax.fori_loop(0, 4, join, 0)
 
     with jax.named_scope("drain"):
-        for c in (0, 1):
+        for d in (0, 1):
             for r in range(4):
-                forward(r, c, drain)
+                forward(r, d, drain)
         for d in (0, 1):
             for cc in (0, 1):
                 for rr in (0, 1):
@@ -414,6 +418,18 @@
             for k in (0, 1):
                 r = row_of(parity_to(p // 2, p % 2), k)
                 deliver(r, 1 - p % 2, 2 * p + k).wait()
+
+
+def hand_over(src, dst, held, in_sem, out_sem):
+    takes = [pltpu.make_async_copy(src.at[i], held.at[i], in_sem.at[i]) for i in range(src.shape[0])]
+    gives = [pltpu.make_async_copy(held.at[i], dst.at[i], out_sem.at[i]) for i in range(src.shape[0])]
+    for take in takes:
+        take.start()
+    for take, give in zip(takes, gives):
+        take.wait()
+        give.start()
+    for give in gives:
+        give.wait()
 
 
 def per_device(fields, surface_mask, w_qkv, w_out, logit_scale, mask_bias, w_up, w_down):
@@ -470,6 +486,18 @@
         name="window_block",
     )(raw, jnp.transpose(surface_mask, (1, 0, 2)), logit_scale, mask_bias, w_qkv, w_out, w_up, w_down)
 
+    joined = pl.pallas_call(
+        hand_over,
+        out_shape=jax.ShapeDtypeStruct(raw.shape, BF16),
+        in_specs=[anywhere],
+        out_specs=anywhere,
+        scratch_shapes=[
+            pltpu.VMEM(raw.shape, BF16),
+            pltpu.SemaphoreType.DMA((groups,)),
+            pltpu.SemaphoreType.DMA((groups,)),
+        ],
+        name="hand_over",
+    )(joined)
     joined = joined.reshape(groups, nlat, nlon, tiles, levels, 128)
     return jnp.transpose(joined, (0, 4, 1, 2, 3, 5)).reshape(fields.shape)
 

time: 51.6 us -> 45.6 us (0.88); the launches traced: 51.3 us -> 44.8 us
  Pallas kernels: 48.6 us -> 44.8 us
  local copies, waits for them, and re-layouts: 2.76 us -> 0 us
    pallas_call x1, Pallas kernels: 48.6 us -> 42.9 us  [per_device(): pl.pallas_call(functools.partial(kernel, real, heads), out_shape=jax.Shap...]
    unnamed x1 -> x0, local copies, waits for them, and re-layouts: 2.76 us -> none
    pallas_call x0 -> x1, Pallas kernels: none -> 1.92 us  [per_device(): pl.pallas_call(hand_over, out_shape=jax.ShapeDtypeStruct(raw.shape, BF16)...]
where the time goes in v4:
time: 45.6 us; the launch traced here: 44.8 us
  Pallas kernels  44.8 us (98%)
    pallas_call x1, Pallas kernels, per_device(): pl.pallas_call(functools.partial(kernel, real, heads), out_shape=jax.Shap...  42.9 us
    pallas_call x1, Pallas kernels, per_device(): pl.pallas_call(hand_over, out_shape=jax.ShapeDtypeStruct(raw.shape, BF16)...  1.92 us

profile of v4, /device:TPU:1, one launch (start us, length us, event | category | flops | bytes accessed | tf_op | source)
XLA Modules:
  0.0 44.8 jit_solution(10122983554866207842)
XLA Ops:
  0.0 42.9 %window_block.1.src = bf16[3,12,6,16,128]{4,3,2,1,0:T(8,128)(2,1)} custom-call(bf16[3,12,6,16,128]{4,3,2,1,0:T(8,128)(2,1)} %bitcast.11, s32[12,2,12]{2,1,0:T(2,128)} %bitcast.12, f32[8]{0:T(128)} %scale_ref.1, f32[8]{0:T(128)} %bias_ref.1, bf16[512,1536]{1,0:T(8,128)(2,1)} %wqkv_hbm.1, bf16[512,512]{1,0:T(8,128)(2,1)} %wout_hbm.1, ...), custom_call_target="tpu_custom_call" | custom-call | tf_op jit(solution)/shard_map/window_block/pallas_call | solution.py:453
  42.9 1.9 %hand_over.1 = bf16[3,12,6,16,128]{4,3,2,1,0:T(8,128)(2,1)} custom-call(bf16[3,12,6,16,128]{4,3,2,1,0:T(8,128)(2,1)} %window_block.1.src), custom_call_target="tpu_custom_call" | custom-call | tf_op jit(solution)/shard_map/hand_over/pallas_call | solution.py:489

commit v5 on v4

--- a/solution.py
+++ b/solution.py
@@ -192,7 +192,6 @@
 
     with jax.named_scope("load"):
         load.wait()
-    order = (0, 3, 1, 2)
 
     def sort_row(r):
         for c in (0, 1):
@@ -207,16 +206,17 @@
                 tall[rows - 16 : rows].astype(F32),
             ).astype(BF16)
 
-    sort_row(order[0])
+    sort_row(0)
     with jax.named_scope("greet"):
         pl.semaphore_wait(barrier, greeted)
-    for k in range(4):
-        if k < 3:
-            sort_row(order[k + 1])
-        forward(order[k], 0, begin)
-        if k:
-            forward(order[k - 1], 1, begin)
-    forward(order[3], 1, begin)
+    for r in range(4):
+        if r < 3:
+            sort_row(r + 1)
+        forward(r, 0, begin)
+        if r > 1:
+            forward(r - 1, 1, begin)
+    forward(0, 1, begin)
+    forward(3, 1, begin)
 
     last = jnp.where(a == na - 1, (g + b) % 2, 0)
     row_in_block = iota((pair_rows, lanes), 0) % rows

time: 45.6 us -> 44.8 us (0.982); the launches traced: 44.8 us -> 44.6 us
  no operation moved by 1% of the time
where the time goes in v5:
time: 44.8 us; the launch traced here: 44.6 us
  Pallas kernels  44.6 us (100%)
    pallas_call x1, Pallas kernels, per_device(): pl.pallas_call(functools.partial(kernel, real, heads), out_shape=jax.Shap...  42.7 us
    pallas_call x1, Pallas kernels, per_device(): pl.pallas_call(hand_over, out_shape=jax.ShapeDtypeStruct(raw.shape, BF16)...  1.92 us

profile of v5, /device:TPU:1, one launch (start us, length us, event | category | flops | bytes accessed | tf_op | source)
XLA Modules:
  0.0 44.6 jit_solution(18258024978908458650)
XLA Ops:
  0.0 42.7 %window_block.1.src = bf16[3,12,6,16,128]{4,3,2,1,0:T(8,128)(2,1)} custom-call(bf16[3,12,6,16,128]{4,3,2,1,0:T(8,128)(2,1)} %bitcast.11, s32[12,2,12]{2,1,0:T(2,128)} %bitcast.12, f32[8]{0:T(128)} %scale_ref.1, f32[8]{0:T(128)} %bias_ref.1, bf16[512,1536]{1,0:T(8,128)(2,1)} %wqkv_hbm.1, bf16[512,512]{1,0:T(8,128)(2,1)} %wout_hbm.1, ...), custom_call_target="tpu_custom_call" | custom-call | tf_op jit(solution)/shard_map/window_block/pallas_call | solution.py:453
  42.7 1.9 %hand_over.1 = bf16[3,12,6,16,128]{4,3,2,1,0:T(8,128)(2,1)} custom-call(bf16[3,12,6,16,128]{4,3,2,1,0:T(8,128)(2,1)} %window_block.1.src), custom_call_target="tpu_custom_call" | custom-call | tf_op jit(solution)/shard_map/hand_over/pallas_call | solution.py:489
